TPU v7x, 32 devices: a whole 2x2x4 slice. The times are simulated.
32 devices in a mesh: tm: 8 (over z, x), pair: 4 (over y, core).
Axes of the slice: x: 2, y: 2, z: 4, core: 2. Of those that a mesh axis runs over, the one named last changes fastest.
Arguments:
- voltages: bfloat16 [2, 32, 262144], P(None, 'pair', 'tm'), may hold values from -3 to 3
- delays: int32 [32, 32], P('pair', 'tm'), may hold values from 0 to 49152, as said below
- phase_model: float32 [32, 8192], replicated, may hold values from -3.140625 to 3.140625
- phase_bins: int32 [32], P('tm'), may hold values from 0 to 31
- assignment: int32 [16], P('pair'), may hold values from 0 to 15, each once
Outputs:
- visibility: float32 [32, 16, 2, 64, 128], P('tm', 'pair')
Inputs may be any that keep to these rules, and one draw needn't show every extreme that they name: `delays`: delay of each station in each recording block of 1 frames; both 0 and 49152 occur in every draw. `assignment`: each of the 16 station-pair blocks occurs once.
All inputs are finite; a program needn't handle non-finite values.
Results may differ from a plain program's by a relative error of at most 0.0085.
Values may be sent and summed in bfloat16 or wider, within the bound.
A program may use at most 128 MiB of HBM per device.

v0:
```python
import functools
import math

import jax
import jax.numpy as jnp
import numpy as np
from jax import lax
from jax.experimental import pallas as pl
from jax.experimental.pallas import tpu as pltpu
from jax.sharding import PartitionSpec as P

NCHAN = 8192
GROUP_ST = 8
RADIX_A = 16
CHAVG = 64
NGRP = 4
OUTCH = 128
BINS = 32
DELAY_MAX = 49152
LANES = 128
RADIX_B = NCHAN // RADIX_A
QUADS = RADIX_B // LANES
F32, BF16 = jnp.float32, jnp.bfloat16
AXES = ("tm", "pair")


def section_tables(stations):
    a, b = np.arange(RADIX_A), np.arange(RADIX_B)
    angle = ((a[:, None] * a[None, :]) % RADIX_A).astype(np.float32) * np.float32(2.0 * math.pi / RADIX_A)
    cos_a = (np.cos(angle) * np.float32(1.0 / math.sqrt(RADIX_A))).astype(np.float32)
    sin_a = (np.sin(angle) * np.float32(1.0 / math.sqrt(RADIX_A))).astype(np.float32)
    small = np.stack([np.stack([cos_a, sin_a], 1), np.stack([-sin_a, cos_a], 1)], 0)
    first = np.einsum("st,pkrn->psktrn", np.eye(stations, dtype=np.float32), small)
    rows = 2 * stations * RADIX_A
    first = first.reshape(rows, rows)
    turn = (a[:, None] * b[None, :]).astype(np.float32) * np.float32(2.0 * math.pi / NCHAN)
    twist = np.stack([np.cos(turn), np.sin(turn)]).astype(np.float32)
    twist = np.tile(twist, (1, stations, 1))
    angle = ((b[:, None] * b[None, :]) % RADIX_B).astype(np.float32) * np.float32(2.0 * math.pi / RADIX_B)
    cos_b = (np.cos(angle) * np.float32(1.0 / math.sqrt(RADIX_B))).astype(np.float32)
    sin_b = (np.sin(angle) * np.float32(1.0 / math.sqrt(RADIX_B))).astype(np.float32)
    second = np.stack([np.stack([cos_b, -sin_b], 1), np.stack([sin_b, cos_b], 1)], 0)
    second = second.reshape(2, RADIX_B, 2, OUTCH, QUADS).transpose(0, 1, 4, 2, 3)
    second = second.reshape(2 * RADIX_B, 2 * RADIX_B)
    return jnp.asarray(first, BF16), jnp.asarray(twist), jnp.asarray(second, BF16)


def spectra_kernel(dims, delays, own, following, beyond, first, twist, second, phase, out,
                   series, windows, turned, planes, rows):
    frames, stations = dims
    held, ahead, last = own.shape[2], following.shape[2], beyond.shape[2]
    sk = stations * RADIX_A

    def widen(s, carry):
        for r in range(2):
            series[r, s, 0:held] = own[r, s].astype(F32)
            series[r, s, held:held + ahead] = following[r, s].astype(F32)
            series[r, s, held + ahead:held + ahead + last] = beyond[r, s].astype(F32)
            series[r, s, held + ahead + last:] = jnp.zeros((8, LANES), F32)
        return carry

    lax.fori_loop(0, stations, widen, 0)
    lane = lax.broadcasted_iota(jnp.int32, (RADIX_A, LANES), 1)

    def one_frame(f, carry):
        for s in range(stations):
            offset = f * NCHAN + delays[s, f]
            row, shift = offset // LANES, offset % LANES
            for r in range(2):
                parts = [
                    pltpu.roll(series[r, s, pl.ds(row + h, RADIX_A, stride=QUADS), :], (LANES - shift) % LANES, 1)
                    for h in range(QUADS + 1)
                ]
                for h in range(QUADS):
                    cut = jnp.where(lane < LANES - shift, parts[h], parts[h + 1])
                    windows[(2 * s + r) * RADIX_A:(2 * s + r + 1) * RADIX_A, h * LANES:(h + 1) * LANES] = cut.astype(BF16)
        passed = jnp.dot(first[...], windows[...], preferred_element_type=F32)
        real, imag = passed[:sk], passed[sk:]
        here = pl.ds(pl.multiple_of(f * sk, sk), sk)
        turned[here, 0:RADIX_B] = (real * twist[0] + imag * twist[1]).astype(BF16)
        turned[here, RADIX_B:] = (imag * twist[0] - real * twist[1]).astype(BF16)
        return carry

    lax.fori_loop(0, frames, one_frame, 0)
    for g in range(QUADS):
        channels = jnp.dot(turned[...], second[:, g * 2 * LANES:(g + 1) * 2 * LANES], preferred_element_type=F32)
        real = channels[:, :LANES].reshape(frames, sk, LANES)
        imag = channels[:, LANES:].reshape(frames, sk, LANES)
        cosine, sine = phase[0, g], phase[1, g]
        turned_re = (real * cosine - imag * sine).reshape(frames * stations, RADIX_A, LANES)
        turned_im = (real * sine + imag * cosine).reshape(frames * stations, RADIX_A, LANES)
        planes[:, g * RADIX_A:(g + 1) * RADIX_A, :] = turned_re
        planes[:, CHAVG + g * RADIX_A:CHAVG + (g + 1) * RADIX_A, :] = turned_im

    count = frames * stations

    def flip(i, carry):
        rows[pl.ds(i, OUTCH, stride=count), :] = planes[i].T
        return carry

    lax.fori_loop(0, count, flip, 0, unroll=4)
    out[...] = rows[...].astype(BF16).reshape(out.shape)


def product_kernel(dims, small, spectra, out, sums):
    owners, pairs, group, slots = dims
    depth, frames = spectra.shape[2], spectra.shape[3]
    pairings = depth // group
    stations = pairs * spectra.shape[4]
    sums[...] = jnp.zeros_like(sums)
    lane = lax.broadcasted_iota(jnp.int32, (stations, LANES), 1)

    def one_owner(t, carry):
        for f in range(frames):
            b = small[t * pairs, f]
            for op in range(pairings):
                grams = []
                for o2 in range(group):
                    held = [spectra[t, p, op * group + o2, f].astype(F32) for p in range(pairs)]
                    left = jnp.concatenate(held, 0)
                    swapped = pltpu.roll(left, CHAVG, 1)
                    swapped = jnp.where(lane < CHAVG, -swapped, swapped)
                    right = jnp.concatenate([left, swapped], 0).astype(BF16)
                    grams.append(lax.dot_general(
                        left.astype(BF16), right, (((1,), (1,)), ((), ())), preferred_element_type=F32))
                if group == 1:
                    grams.append(jnp.zeros_like(grams[0]))
                sums[b, op] += jnp.concatenate(grams, 1)
        return carry

    lax.fori_loop(0, owners, one_owner, 0)
    width = slots * 2 * GROUP_ST
    source = lax.broadcasted_iota(jnp.int32, (LANES, LANES), 0)
    target = lax.broadcasted_iota(jnp.int32, (LANES, LANES), 1)
    slot_of = (target // (2 * GROUP_ST)) % slots
    wanted = (target // width) * (2 * stations) + (target // GROUP_ST) % 2 * stations + target % GROUP_ST
    inside = target < group * width
    total = sums.shape[0] * pairings * GROUP_ST
    for p in range(pairs):
        moved = jnp.zeros((total, LANES), F32)
        for k in range(slots):
            block = small[p, frames + k]
            top = pl.multiple_of(block // NGRP * GROUP_ST, GROUP_ST)
            left = block % NGRP * GROUP_ST
            lines = sums[:, :, pl.ds(top, GROUP_ST), :].reshape(total, LANES)
            pick = (source == wanted + left) & (slot_of == k) & inside
            moved += jnp.dot(
                (lines * (1.0 / CHAVG)).astype(BF16),
                jnp.where(pick, 1.0, 0.0).astype(BF16),
                preferred_element_type=F32)
        out[:, p] = moved.reshape(owners, -1, pairings * GROUP_ST, LANES).astype(BF16)


def place_kernel(dims, received, out, lines):
    replicas, depth, group = dims
    count, here, rows_of = received.shape[0], received.shape[1], received.shape[2]
    pairings = rows_of // GROUP_ST
    slots = out.shape[1]
    width = slots * 2 * GROUP_ST
    lines[...] = received[...].reshape(lines.shape).astype(F32)
    row = lax.broadcasted_iota(jnp.int32, (pairings * count, OUTCH), 0)
    lane = lax.broadcasted_iota(jnp.int32, (pairings * count, OUTCH), 1)
    device, op = row % count, row // count
    places = []
    for o2 in range(group):
        channel = device // replicas * depth + op * group + o2
        hit = (channel == lane) & (device % replicas == 0)
        places.append(jnp.where(hit, 1.0, 0.0).astype(BF16))

    def one(step, carry):
        b, p = step // GROUP_ST, step % GROUP_ST
        sent = [
            lines[pl.ds(b * rows_of + op * GROUP_ST + p, count, stride=here * rows_of), :]
            for op in range(pairings)
        ]
        sent = jnp.concatenate(sent, 0)
        value = jnp.zeros((width, OUTCH), F32)
        for o2 in range(group):
            part = sent[:, o2 * width:(o2 + 1) * width].astype(BF16)
            value += lax.dot_general(
                part, places[o2], (((0,), (0,)), ((), ())), preferred_element_type=F32)
        value = value.reshape(slots, 2, GROUP_ST, OUTCH)
        out[b, :, :, pl.ds(pl.multiple_of(p * GROUP_ST, GROUP_ST), GROUP_ST), :] = value
        return carry

    lax.fori_loop(0, here * GROUP_ST, one, 0, unroll=8)


VMEM = pl.BlockSpec(memory_space=pltpu.VMEM)
SMEM = pl.BlockSpec(memory_space=pltpu.SMEM)
PARAMS = pltpu.CompilerParams(vmem_limit_bytes=48 * 1024 * 1024)


def from_behind(value, axis, steps):
    count = lax.axis_size(axis)
    first, last = (max(0, -steps), min(count, count - steps))
    return lax.ppermute(value, axis, [(source, source + steps) for source in range(first, last)])


def exchange_kernel(dims, shared, *refs):
    owners, pairs = dims
    devices = owners * pairs
    buffers = 2 if shared else 1
    sources, targets = refs[:buffers], refs[buffers:2 * buffers]
    send_sems, recv_sems, own_sems = refs[2 * buffers:]
    me = lax.axis_index("tm") * pairs + lax.axis_index("pair")
    barrier = pltpu.get_barrier_semaphore()

    def place_of(device):
        return (device // pairs, device % pairs)

    def greet(step, carry):
        peer = (me + step) % devices
        pl.semaphore_signal(barrier, inc=1, device_id=place_of(peer), device_id_type=pl.DeviceIdType.MESH)
        return carry

    lax.fori_loop(1, devices, greet, 0)
    pl.semaphore_wait(barrier, devices - 1)

    def piece(which, device):
        return sources[0].at[device] if which == 0 else sources[1]

    def copies(step, peer, slot):
        return [
            pltpu.make_async_remote_copy(
                src_ref=piece(which, peer), dst_ref=targets[which].at[slot],
                send_sem=send_sems.at[which, step], recv_sem=recv_sems.at[which, step],
                device_id=place_of(peer), device_id_type=pl.DeviceIdType.MESH)
            for which in range(buffers)
        ]

    def start(step, carry):
        for copy in copies(step, (me + step) % devices, me):
            copy.start()
        return carry

    lax.fori_loop(1, devices, start, 0)
    for which in range(buffers):
        own = pltpu.make_async_copy(piece(which, me), targets[which].at[me], own_sems.at[which])
        own.start()
        own.wait()

    def finish(step, carry):
        for copy in copies(step, (me + step) % devices, me):
            copy.wait_send()
        source = (me + devices - step) % devices
        for copy in copies(step, source, source):
            copy.wait_recv()
        return carry

    lax.fori_loop(1, devices, finish, 0)


def exchange(value, number, shared=None):
    owners, pairs = lax.axis_size("tm"), lax.axis_size("pair")
    devices = owners * pairs
    shapes = [jax.ShapeDtypeStruct(value.shape, value.dtype)]
    values = [value]
    if shared is not None:
        shapes.append(jax.ShapeDtypeStruct((devices,) + shared.shape, shared.dtype))
        values.append(shared)
    result = pl.pallas_call(
        functools.partial(exchange_kernel, (owners, pairs), shared is not None),
        out_shape=shapes,
        in_specs=[VMEM] * len(values),
        out_specs=[VMEM] * len(values),
        scratch_shapes=[
            pltpu.SemaphoreType.DMA((len(values), devices)),
            pltpu.SemaphoreType.DMA((len(values), devices)),
            pltpu.SemaphoreType.DMA((len(values),)),
        ],
        compiler_params=pltpu.CompilerParams(collective_id=number, has_side_effects=True),
        name="exchange",
    )(*values)
    return result if shared is not None else result[0]


def body(voltages, delays, phase_model, phase_bins, assignment):
    owners, pairs = lax.axis_size("tm"), lax.axis_size("pair")
    devices = owners * pairs
    stations, samples = voltages.shape[1], voltages.shape[2]
    frames = samples // NCHAN
    slots = assignment.shape[0]
    channel_groups = min(devices, OUTCH)
    depth = OUTCH // channel_groups
    replicas = devices // channel_groups
    group = min(2, depth)
    count = frames * stations

    first, twist, second = section_tables(stations)
    lines = voltages.reshape(2, stations, samples // LANES, LANES)
    ahead = min(DELAY_MAX, samples)
    last = DELAY_MAX - ahead
    following = from_behind(lines[:, :, :ahead // LANES], "tm", -1)
    beyond = from_behind(lines[:, :, :last // LANES], "tm", -2)

    angles = lax.dynamic_slice_in_dim(phase_model, lax.axis_index("pair") * stations, stations, 0)
    angles = angles.reshape(stations, OUTCH, QUADS, RADIX_A).transpose(2, 0, 3, 1)
    angles = angles.reshape(QUADS, stations * RADIX_A, OUTCH)
    phase = jnp.stack([jnp.cos(angles), jnp.sin(angles)])

    total_rows = (samples + DELAY_MAX) // LANES + 8
    sk = stations * RADIX_A
    spectra = pl.pallas_call(
        functools.partial(spectra_kernel, (frames, stations)),
        out_shape=jax.ShapeDtypeStruct((OUTCH, count, LANES), BF16),
        in_specs=[SMEM] + [VMEM] * 7,
        out_specs=VMEM,
        scratch_shapes=[
            pltpu.VMEM((2, stations, total_rows, LANES), F32),
            pltpu.VMEM((2 * sk, RADIX_B), BF16),
            pltpu.VMEM((frames * sk, 2 * RADIX_B), BF16),
            pltpu.VMEM((count, LANES, LANES), F32),
            pltpu.VMEM((OUTCH * count, LANES), F32),
        ],
        compiler_params=PARAMS,
        name="spectra",
    )(delays, lines, following, beyond, first, twist, second, phase)

    sent = spectra.reshape(channel_groups, depth * count, LANES)
    if replicas > 1:
        sent = jnp.repeat(sent, replicas, axis=0)
    own_small = jnp.concatenate([phase_bins, assignment])
    own_small = jnp.pad(own_small, (0, LANES - own_small.shape[0])).reshape(1, LANES)
    routed, small = exchange(sent, 0, own_small)
    small = small[:, 0, :frames + slots]
    routed = routed.reshape(owners, pairs, depth, frames, stations, LANES)

    all_bins = BINS
    bins_here = all_bins // owners
    rows_of = depth // group * GROUP_ST
    binned = pl.pallas_call(
        functools.partial(product_kernel, (owners, pairs, group, slots)),
        out_shape=jax.ShapeDtypeStruct((owners, pairs, bins_here, rows_of, LANES), BF16),
        in_specs=[SMEM, VMEM],
        out_specs=VMEM,
        scratch_shapes=[pltpu.VMEM((all_bins, depth // group, pairs * stations, LANES), F32)],
        compiler_params=PARAMS,
        name="products",
    )(small, routed)

    returned = exchange(binned.reshape(devices, bins_here, rows_of, LANES), 1)
    return pl.pallas_call(
        functools.partial(place_kernel, (replicas, depth, group)),
        out_shape=jax.ShapeDtypeStruct((bins_here, slots, 2, GROUP_ST * GROUP_ST, OUTCH), F32),
        in_specs=[VMEM],
        out_specs=VMEM,
        scratch_shapes=[pltpu.VMEM((devices * bins_here * rows_of, LANES), F32)],
        compiler_params=PARAMS,
        name="place",
    )(returned)


def solution(mesh):
    in_specs = (P(None, "pair", "tm"), P("pair", "tm"), P(), P("tm"), P("pair"))
    out_specs = P("tm", "pair", None, None, None)
    return jax.shard_map(body, mesh=mesh, in_specs=in_specs, out_specs=out_specs, check_vma=False)
```

profile of v0, /device:TPU:0, one launch (start us, length us, event | category | flops | bytes accessed | tf_op | source)
XLA Modules:
  0.0 108.7 jit_solution(4826311064824540584)
XLA Ops:
  0.0 1.4 %copy.19 = bf16[2,8,256,128]{3,2,1,0:T(8,128)(2,1)S(1)} copy(bf16[2,8,256,128]{3,1,2,0:T(8,128)(2,1)} %bitcast.23) | data formatting | bytes 2097152
  1.4 1.3 %collective-permute-start = (bf16[2,8,256,128]{3,2,1,0:T(8,128)(2,1)S(1)}, bf16[2,8,256,128]{3,2,1,0:T(8,128)(2,1)S(1)}, u32[]{:S(2)}, u32[]{:S(2)}) collective-permute-start(bf16[2,8,256,128]{3,2,1,0:T(8,128)(2,1)S(1)} %copy.19), channel_id=1, source_target_pairs={{4,0},{8,4},{12,8},{16,12},{20,16},{24,20},{28,24},{5,1},{9,5},{13... | collective-permute-start | bytes 3145736 | tf_op jit(solution)/shard_map/ppermute | solution.py:197
  2.7 0.8 slice.8
  3.6 1.3 %collective-permute-start.1 = (bf16[2,8,128,128]{3,2,1,0:T(8,128)(2,1)}, bf16[2,8,128,128]{3,2,1,0:T(8,128)(2,1)S(1)}, u32[]{:S(2)}, u32[]{:S(2)}) collective-permute-start(bf16[2,8,128,128]{3,2,1,0:T(8,128)(2,1)} %slice.8), channel_id=1, source_target_pairs={{8,0},{12,4},{16,8},{20,12},{24,16},{28,20},{9,1},{13,5},{17,9},{2... | collective-permute-start | bytes 1572872 | tf_op jit(solution)/shard_map/ppermute | solution.py:197
  4.8 1.9 %dynamic-slice_cosine_fusion = (f32[8,8192]{1,0:T(8,128)S(1)}, f32[8,8192]{1,0:T(8,128)S(1)}) fusion(f32[32,8192]{1,0:T(8,128)} %param.10, s32[]{:T(128)S(6)} %select_n.3), kind=kLoop, calls=%fused_computation.3 | loop fusion | bytes 786436 | tf_op jit(solution)/shard_map/cos | solution.py:300
  6.7 2.8 %cos.20 = f32[8,128,4,16]{3,2,1,0:T(4,128)} reshape(f32[8,8192]{1,0:T(8,128)S(1)} %get-tuple-element.9) | data formatting | bytes 524288 | tf_op jit(solution)/shard_map/cos | solution.py:300
  9.5 1.8 %copy.13 = f32[4,8,16,128]{3,2,1,0:T(8,128)S(1)} copy(f32[4,8,16,128]{2,0,3,1:T(4,128)} %bitcast.21) | data formatting | bytes 524288 | tf_op jit(solution)/shard_map/cos | solution.py:300
  11.4 0.0 copy-start.6
  11.4 0.0 copy-start.7
  11.4 0.0 copy-start.8
  11.4 2.8 %sin.20 = f32[8,128,4,16]{3,2,1,0:T(4,128)} reshape(f32[8,8192]{1,0:T(8,128)S(1)} %get-tuple-element.10) | data formatting | bytes 524288 | tf_op jit(solution)/shard_map/sin | solution.py:300
  14.2 0.0 copy-start.4
  14.2 0.0 copy-start.5
  14.2 2.6 %copy.14 = f32[4,8,16,128]{3,2,1,0:T(8,128)} copy(f32[4,8,16,128]{2,0,3,1:T(4,128)} %bitcast.22) | data formatting | bytes 524288 | tf_op jit(solution)/shard_map/sin | solution.py:300
  16.8 0.0 copy-done.6
  16.8 0.1 copy.15.delays
  16.9 0.0 copy-done.7
  16.9 0.0 copy-done.8
  16.9 0.1 pad_add_fusion
  16.9 0.5 pad_bitcast_fusion.refs_1_
  17.5 1.0 pad_maximum_fusion.phase
  18.4 23.4 %collective-permute-done.1.beyond = bf16[2,8,128,128]{3,2,1,0:T(8,128)(2,1)S(1)} collective-permute-done((bf16[2,8,128,128]{3,2,1,0:T(8,128)(2,1)}, bf16[2,8,128,128]{3,2,1,0:T(8,128)(2,1)S(1)}, u32[]{:S(2)}, u32[]{:S(2)}) %collective-permute-start.1) | collective-permute-done | bytes 524320 | tf_op jit(solution)/shard_map/ppermute | solution.py:197
  41.8 0.0 collective-permute-done.following
  41.8 0.0 copy-done.4
  41.9 0.0 copy-done.5
  41.9 6.9 %spectra.1 = bf16[128,32,128]{2,1,0:T(8,128)(2,1)S(1)} custom-call(s32[8,4]{1,0:T(8,128)S(1)} %copy.15.delays, bf16[2,8,256,128]{3,2,1,0:T(8,128)(2,1)S(1)} %copy.19, bf16[2,8,256,128]{3,2,1,0:T(8,128)(2,1)S(1)} %collective-permute-done.following, bf16[2,8,128,128]{3,2,1,0:T(8,128)(2,1)S(1)} %collective-permute-done.1.beyond, ...), custom_call_target="tpu_custom_call" | custom-call | tf_op jit(solution)/shard_map/spectra/pallas_call | solution.py:304
  48.8 0.0 copy-start
  48.8 1.0 copy-done
  49.8 24.6 %exchange.2 = (bf16[32,128,128]{2,1,0:T(8,128)(2,1)}, s32[32,1,128]{2,1,0:T(1,128)}) custom-call(bf16[32,128,128]{2,1,0:T(8,128)(2,1)} %bitcast.18, s32[1,128]{1,0:T(1,128)} %pad_bitcast_fusion.refs_1_), custom_call_target="tpu_custom_call" | custom-call | tf_op jit(solution)/shard_map/exchange/pallas_call | solution.py:262
  74.4 0.7 slice_bitcast_fusion.small
  75.1 0.0 copy-start.3
  75.1 1.2 %copy-done.3 = bf16[32,128,128]{2,1,0:T(8,128)(2,1)S(1)} copy-done((bf16[32,128,128]{2,1,0:T(8,128)(2,1)S(1)}, bf16[32,128,128]{2,1,0:T(8,128)(2,1)}, u32[]{:S(2)}) %copy-start.3) | copy-done | bytes 1048600
  76.4 4.7 %products.1 = bf16[8,4,4,16,128]{4,3,2,1,0:T(8,128)(2,1)S(1)} custom-call(s32[32,8]{1,0:T(8,128)S(1)} %slice_bitcast_fusion.small, bf16[8,4,4,4,8,128]{5,4,3,2,1,0:T(8,128)(2,1)S(1)} %bitcast.20), custom_call_target="tpu_custom_call" | custom-call | tf_op jit(solution)/shard_map/products/pallas_call | solution.py:332
  81.0 0.0 copy-start.1
  81.1 0.8 copy-done.1
  81.8 22.9 %exchange.3.received = bf16[32,4,16,128]{3,2,1,0:T(8,128)(2,1)} custom-call(bf16[32,4,16,128]{3,2,1,0:T(8,128)(2,1)} %bitcast.19), custom_call_target="tpu_custom_call" | custom-call | tf_op jit(solution)/shard_map/exchange/pallas_call | solution.py:262
  104.8 0.0 copy-start.2
  104.8 1.0 copy-done.2
  105.8 2.9 %place.1 = f32[4,4,2,64,128]{4,3,2,1,0:T(8,128)} custom-call(bf16[32,4,16,128]{3,2,1,0:T(8,128)(2,1)S(1)} %copy-done.2), custom_call_target="tpu_custom_call" | custom-call | tf_op jit(solution)/shard_map/place/pallas_call | solution.py:343
Async XLA Ops:
  1.4 40.4 %collective-permute-start = (bf16[2,8,256,128]{3,2,1,0:T(8,128)(2,1)S(1)}, bf16[2,8,256,128]{3,2,1,0:T(8,128)(2,1)S(1)}, u32[]{:S(2)}, u32[]{:S(2)}) collective-permute-start(bf16[2,8,256,128]{3,2,1,0:T(8,128)(2,1)S(1)} %copy.19), channel_id=1, source_target_pairs={{4,0},{8,4},{12,8},{16,12},{20,16},{24,20},{28,24},{5,1},{9,5},{13... | collective-permute-start | bytes 3145736 | tf_op jit(solution)/shard_map/ppermute | solution.py:197
  3.6 38.3 %collective-permute-start.1 = (bf16[2,8,128,128]{3,2,1,0:T(8,128)(2,1)}, bf16[2,8,128,128]{3,2,1,0:T(8,128)(2,1)S(1)}, u32[]{:S(2)}, u32[]{:S(2)}) collective-permute-start(bf16[2,8,128,128]{3,2,1,0:T(8,128)(2,1)} %slice.8), channel_id=1, source_target_pairs={{8,0},{12,4},{16,8},{20,12},{24,16},{28,20},{9,1},{13,5},{17,9},{2... | collective-permute-start | bytes 1572872 | tf_op jit(solution)/shard_map/ppermute | solution.py:197
  11.4 5.4 %copy-start.6 = (s32[8,4]{0,1:T(4,128)S(1)}, s32[8,4]{0,1:T(4,128)}, u32[]{:S(2)}) copy-start(s32[8,4]{0,1:T(4,128)} %param.9) | copy-start | bytes 388
  11.4 5.5 %copy-start.7 = (s32[4]{0:T(128)S(1)}, s32[4]{0:T(128)}, u32[]{:S(2)}) copy-start(s32[4]{0:T(128)} %param.12) | copy-start | bytes 52
  11.4 5.5 %copy-start.8 = (s32[4]{0:T(128)S(1)}, s32[4]{0:T(128)}, u32[]{:S(2)}) copy-start(s32[4]{0:T(128)} %param.11) | copy-start | bytes 52
  14.2 27.6 %copy-start.4 = (f32[2,128,512]{2,1,0:T(8,128)S(1)}, f32[2,128,512]{2,1,0:T(8,128)}, u32[]{:S(2)}) copy-start(f32[2,128,512]{2,1,0:T(8,128)} %constant.17.clone.twist) | copy-start | bytes 1572868
  14.2 27.6 %copy-start.5 = (bf16[256,256]{1,0:T(8,128)(2,1)S(1)}, bf16[256,256]{1,0:T(8,128)(2,1)}, u32[]{:S(2)}) copy-start(bf16[256,256]{1,0:T(8,128)(2,1)} %constant.16.clone.first) | copy-start | bytes 393220
  48.8 1.0 copy-start
  75.1 1.2 %copy-start.3 = (bf16[32,128,128]{2,1,0:T(8,128)(2,1)S(1)}, bf16[32,128,128]{2,1,0:T(8,128)(2,1)}, u32[]{:S(2)}) copy-start(bf16[32,128,128]{2,1,0:T(8,128)(2,1)} %get-tuple-element.8) | copy-start | bytes 3145732
  81.0 0.8 copy-start.1
  104.8 1.0 copy-start.2
where the time goes:
time: 111 us; the launch traced here: 109 us
  Pallas kernels  62.1 us (56%)
  waiting for transfers between devices  23.4 us (21%)
  local copies, waits for them, and re-layouts  19.5 us (18%)
  starting transfers between devices  2.57 us (2%)
    pallas_call x2, Pallas kernels, exchange(): pl.pallas_call(functools.partial(exchange_kernel, (owners, pairs), shared...  47.6 us
    ppermute x2, waiting for transfers between devices, from_behind(): lax.ppermute(value, axis, [(source, source + steps) for source in range(f...  23.4 us
    pallas_call x1, Pallas kernels, body(): pl.pallas_call(functools.partial(spectra_kernel, (frames, stations)), out...  6.93 us
    cos x3, local copies, waits for them, and re-layouts, body(): phase = jnp.stack([jnp.cos(angles), jnp.sin(angles)])  6.51 us
    unnamed x20, local copies, waits for them, and re-layouts  5.52 us
    sin x2, local copies, waits for them, and re-layouts, body(): phase = jnp.stack([jnp.cos(angles), jnp.sin(angles)])  5.38 us
    pallas_call x1, Pallas kernels, body(): pl.pallas_call(functools.partial(product_kernel, (owners, pairs, group, s...  4.68 us
    pallas_call x1, Pallas kernels, body(): pl.pallas_call(functools.partial(place_kernel, (replicas, depth, group)),...  2.92 us
  transfers between devices with their start and end apart: 2, of which 1 were waited for; matrix products, arithmetic and copies ran while one was open for 13% of the time, Pallas kernels for 0%

commit v1 on v0

v1 whole, which is shorter than its diff:
```python
import functools
import math

import jax
import jax.numpy as jnp
import numpy as np
from jax import lax
from jax.experimental import pallas as pl
from jax.experimental.pallas import tpu as pltpu
from jax.sharding import PartitionSpec as P

NCHAN = 8192
GROUP_ST = 8
RADIX_A = 16
CHAVG = 64
NGRP = 4
NBLK = 16
OUTCH = 128
BINS = 32
DELAY_MAX = 49152
LANES = 128
RADIX_B = NCHAN // RADIX_A
QUADS = RADIX_B // LANES
UNIT = NCHAN // LANES
AHEAD = DELAY_MAX // NCHAN
SLICES = GROUP_ST * GROUP_ST // 2
F32, BF16, I32 = jnp.float32, jnp.bfloat16, jnp.int32
MESH = pl.DeviceIdType.MESH


def section_tables(stations):
    a, b = np.arange(RADIX_A), np.arange(RADIX_B)
    angle = ((a[:, None] * a[None, :]) % RADIX_A).astype(np.float32) * np.float32(2.0 * math.pi / RADIX_A)
    cos_a = (np.cos(angle) * np.float32(1.0 / math.sqrt(RADIX_A))).astype(np.float32)
    sin_a = (np.sin(angle) * np.float32(1.0 / math.sqrt(RADIX_A))).astype(np.float32)
    small = np.stack([np.stack([cos_a, sin_a], 1), np.stack([-sin_a, cos_a], 1)], 0)
    first = np.einsum("st,pkrn->psktrn", np.eye(stations, dtype=np.float32), small)
    rows = 2 * stations * RADIX_A
    first = first.reshape(rows, rows)
    turn = (a[:, None] * b[None, :]).astype(np.float32) * np.float32(2.0 * math.pi / NCHAN)
    twist = np.stack([np.cos(turn), np.sin(turn)]).astype(np.float32)
    twist = np.tile(twist, (1, stations, 1))
    angle = ((b[:, None] * b[None, :]) % RADIX_B).astype(np.float32) * np.float32(2.0 * math.pi / RADIX_B)
    cos_b = (np.cos(angle) * np.float32(1.0 / math.sqrt(RADIX_B))).astype(np.float32)
    sin_b = (np.sin(angle) * np.float32(1.0 / math.sqrt(RADIX_B))).astype(np.float32)
    second = np.stack([np.stack([cos_b, -sin_b], 1), np.stack([sin_b, cos_b], 1)], 0)
    second = second.reshape(2, RADIX_B, 2, OUTCH // 2, 2, QUADS).transpose(0, 1, 5, 2, 4, 3)
    second = second.reshape(2 * RADIX_B, 2 * RADIX_B)
    return jnp.asarray(first, BF16), jnp.asarray(twist), jnp.asarray(second, BF16)


def sin_cos(x):
    turns = jnp.round(x * (2.0 / math.pi))
    r = x - turns * 1.5703125
    r = r - turns * 4.837512969970703125e-4
    r = r - turns * 7.54978995489188216e-8
    z = r * r
    s = r + r * z * ((-1.9515295891e-4 * z + 8.3321608736e-3) * z - 1.6666654611e-1)
    c = 1.0 - 0.5 * z + z * z * ((2.443315711809948e-5 * z - 1.388731625493765e-3) * z + 4.166664568298827e-2)
    size = jnp.abs(turns)
    odd = size == 1.0
    far = size == 2.0
    sine = jnp.where(odd, c, s)
    cosine = jnp.where(odd, s, c)
    sine = jnp.where(far | (turns == -1.0), -sine, sine)
    cosine = jnp.where(far | (turns == 1.0), -cosine, cosine)
    return sine, cosine


def fused_kernel(dims, delays, phase_bins, assignment, voltages, phase_model, first_hbm, twist_hbm, second_hbm, out,
                 small, first, twist, second, rxu, series, windows, turned, planes, rows, phases, phase_rows, trig,
                 tx2, rx2, gs, tscr, tx3, rx3, sums, binned, tx4, rx4, landed, rx0, heard, tables, orders,
                 load_sems, s0, r0, s1, r1, s2, r2, s3, r3, s4, r4, own_sems, unit_sems):
    owners, pairs, frames, stations, slots = dims
    devices, layers, halves = owners * pairs, owners // 2, pairs // 2
    all_frames = owners * frames
    bins_here = BINS // owners
    piece = bins_here * 4
    sk = stations * RADIX_A
    depth = (frames + AHEAD) * UNIT + 8
    tm, pair = lax.axis_index("tm"), lax.axis_index("pair")
    u, h, m, c = tm // 2, tm % 2, pair // 2, pair % 2
    me = tm * pairs + pair
    mine = 2 * m + h
    e = h * halves + m
    top = u == layers - 1

    def place_of(device):
        return (device // pairs, device % pairs)

    def remote(src, dst, send_sem, recv_sem, where):
        return pltpu.make_async_remote_copy(
            src_ref=src, dst_ref=dst, send_sem=send_sem, recv_sem=recv_sem, device_id=where, device_id_type=MESH)

    loads = [
        pltpu.make_async_copy(first_hbm, first, load_sems.at[0]),
        pltpu.make_async_copy(twist_hbm, twist, load_sems.at[1]),
        pltpu.make_async_copy(second_hbm, second, load_sems.at[2]),
        pltpu.make_async_copy(
            phase_model.at[pl.ds(pl.multiple_of(mine * stations // 8 * 8, 8), 8)], phases, load_sems.at[3]),
    ]
    for copy in loads:
        copy.start()

    lane = lax.broadcasted_iota(I32, (1, LANES), 1)
    listed, marked = jnp.zeros((1, LANES), I32), jnp.zeros((1, LANES), I32)
    for i in range(stations * frames):
        listed = jnp.where(lane == i, delays[i // frames, i % frames], listed)
    for i in range(frames):
        listed = jnp.where(lane == stations * frames + i, phase_bins[i], listed)
        marked = jnp.where(lane == tm * frames + i, phase_bins[i] + 1, marked)
    for i in range(slots):
        listed = jnp.where(lane == (stations + 1) * frames + i, assignment[i], listed)
    small[0:1] = listed
    small[1:2] = marked

    barrier = pltpu.get_barrier_semaphore()

    def greet(step, carry):
        pl.semaphore_signal(barrier, inc=1, device_id=place_of((me + step) % devices), device_id_type=MESH)
        return carry

    lax.fori_loop(1, devices, greet, 0)
    pl.semaphore_wait(barrier, devices - 1)

    def small_copy(step, peer, slot):
        return remote(small, rx0.at[slot], s0.at[step], r0.at[slot], place_of(peer))

    def start_small(step, carry):
        small_copy(step, (me + step) % devices, me).start()
        return carry

    lax.fori_loop(1, devices, start_small, 0)
    own_small = pltpu.make_async_copy(small, rx0.at[me], own_sems.at[0])
    own_small.start()

    def at(layer, half, core):
        return (2 * layer + half, 2 * m + core)

    def sample_copy(index, src, where, slot):
        return remote(src, rxu.at[slot], s1.at[index], r1.at[slot], where)

    def own_unit(i):
        return voltages.at[:, :, pl.ds(i * NCHAN, NCHAN)]

    def arrived(slot):
        sample_copy(0, rxu.at[slot], at(u, h, c), slot).wait_recv()

    below = u > 0
    lower = jnp.maximum(u - 1, 0)
    is00, is10 = (h == 0) & (c == 0), (h == 1) & (c == 0)
    is01, is11 = (h == 0) & (c == 1), (h == 1) & (c == 1)
    start_00 = [(0, 0, (lower, 0, 0), 8), (1, 1, (lower, 0, 0), 9), (2, 2, (lower, 0, 1), 6), (3, 3, (lower, 0, 1), 7)]

    @pl.when(is10)
    def _():
        for i in range(4):
            sample_copy(i, own_unit(i), at(u, 0, 0), 4 + i).start()

    @pl.when(is01)
    def _():
        for i in range(4):
            sample_copy(i, own_unit(i), at(u, 1, 0), i).start()

    @pl.when(is11)
    def _():
        for i in range(4):
            sample_copy(i, own_unit(i), at(u, 1, 0), 4 + i).start()

        @pl.when(below)
        def _():
            for i in range(2):
                sample_copy(4 + i, own_unit(i), at(lower, 1, 1), 8 + i).start()

    @pl.when(c == h)
    def _():
        for i in range(4):
            pltpu.make_async_copy(own_unit(i), rxu.at[i], unit_sems.at[i]).start()

    @pl.when(is00 & below)
    def _():
        for index, i, where, slot in start_00:
            sample_copy(index, own_unit(i), at(*where), slot).start()

    for copy in loads:
        copy.wait()

    def spread(j, carry):
        phase_rows[pl.ds(j, 8, stride=UNIT), :] = phases[:, pl.ds(pl.multiple_of(j * LANES, LANES), LANES)]
        return carry

    lax.fori_loop(0, UNIT, spread, 0)
    skip = mine * stations % 8

    def one_phase(s, carry):
        held = phase_rows[pl.ds(pl.multiple_of((skip + s) * UNIT, UNIT), UNIT), :].T
        angles = jnp.concatenate([held[:CHAVG], held[CHAVG:]], 1)
        sine, cosine = sin_cos(angles)
        here = pl.ds(pl.multiple_of(s * RADIX_A, RADIX_A), RADIX_A)
        for g in range(QUADS):
            trig[0, g, here, :] = cosine[g * RADIX_A:(g + 1) * RADIX_A]
            trig[1, g, here, :] = sine[g * RADIX_A:(g + 1) * RADIX_A]
        return carry

    lax.fori_loop(0, stations, one_phase, 0)

    own_small.wait()

    def finish_small(step, carry):
        source = (me + devices - step) % devices
        small_copy(step, source, source).wait_recv()
        return carry

    lax.fori_loop(1, devices, finish_small, 0)
    hear = pltpu.make_async_copy(rx0, heard, own_sems.at[1])
    hear.start()
    hear.wait()
    delays_at = ((2 * u + c) * pairs + 2 * m + h)

    line = rx0[0, 1:2, :]
    for t in range(1, owners):
        line = line + rx0[t * pairs, 1:2, :]
    span = jnp.broadcast_to(line, (all_frames, LANES))
    across = lax.broadcasted_iota(I32, (all_frames, LANES), 1)
    down = lax.broadcasted_iota(I32, (all_frames, LANES), 0)
    column = jnp.max(jnp.where(across == down, span, 0), 1, keepdims=True)
    found = jnp.max(jnp.where((span == column) & (across < down), across, -1), 1, keepdims=True)
    tables[0:all_frames] = jnp.broadcast_to(jnp.where(found < 0, all_frames, found), (all_frames, LANES))
    down = lax.broadcasted_iota(I32, (BINS, LANES), 0)
    across = lax.broadcasted_iota(I32, (BINS, LANES), 1)
    found = jnp.max(jnp.where(jnp.broadcast_to(line, (BINS, LANES)) == down + 1, across, -1), 1, keepdims=True)
    tables[all_frames:] = jnp.broadcast_to(jnp.where(found < 0, all_frames, found), (BINS, LANES))
    tell = pltpu.make_async_copy(tables, orders, own_sems.at[5])
    tell.start()

    def widen(slot):
        def one(j, carry):
            for r in range(2):
                held = rxu[slot, r, :, pl.ds(pl.multiple_of(j * LANES, LANES), LANES)].astype(F32)
                series[pl.ds(r * stations * depth + slot * UNIT + j, stations, stride=depth), :] = held
            return carry
        lax.fori_loop(0, UNIT, one, 0, unroll=4)

    def blank(slot):
        def one(i, carry):
            series[pl.ds(pl.multiple_of(i * depth + slot * UNIT, 8), UNIT), :] = jnp.zeros((UNIT, LANES), F32)
            return carry
        lax.fori_loop(0, 2 * stations, one, 0)

    def clear_tail(i, carry):
        series[pl.ds(pl.multiple_of(i * depth + (frames + AHEAD) * UNIT, 8), 8), :] = jnp.zeros((8, LANES), F32)
        return carry

    lax.fori_loop(0, 2 * stations, clear_tail, 0)

    @pl.when(is00)
    def _():
        for slot in range(4):
            pltpu.make_async_copy(own_unit(slot), rxu.at[slot], unit_sems.at[slot]).wait()
            widen(slot)
        for slot in range(4, 8):
            arrived(slot)
            sample_copy(4 + slot, rxu.at[slot], at(u, 0, 1), slot - 4).start()
            if slot < 6:
                @pl.when(below)
                def _(slot=slot):
                    sample_copy(slot, rxu.at[slot], at(lower, 0, 1), slot + 4).start()

                @pl.when(jnp.logical_not(top))
                def _(slot=slot):
                    arrived(slot + 4)
                    sample_copy(slot + 8, rxu.at[slot + 4], at(u, 0, 1), slot).start()
                    widen(slot + 4)
            widen(slot)

    @pl.when(is10)
    def _():
        for slot in range(4):
            arrived(slot)

            @pl.when(below)
            def _(slot=slot):
                where = at(lower, 1, 0) if slot < 2 else at(lower, 1, 1)
                sample_copy(4 + slot, rxu.at[slot], where, 8 + slot if slot < 2 else 4 + slot).start()
            if slot >= 2:
                @pl.when(jnp.logical_not(top))
                def _(slot=slot):
                    arrived(slot + 6)
                    sample_copy(slot + 6, rxu.at[slot + 6], at(u, 1, 1), slot + 2).start()
                    widen(slot + 6)
            widen(slot)
        for slot in range(4, 8):
            arrived(slot)
            widen(slot)

    @pl.when(is01)
    def _():
        for slot in range(4):
            arrived(slot)
            widen(slot)

    @pl.when(is11)
    def _():
        for slot in range(4):
            pltpu.make_async_copy(own_unit(slot), rxu.at[slot], unit_sems.at[slot]).wait()
            widen(slot)

    @pl.when((c == 1) & jnp.logical_not(top))
    def _():
        for slot in range(4, 8):
            arrived(slot)
            widen(slot)

    @pl.when((c == 1) & top)
    def _():
        for slot in range(4, 8):
            blank(slot)

    @pl.when(top)
    def _():
        for slot in range(8, 10):
            blank(slot)

    lane16 = lax.broadcasted_iota(I32, (RADIX_A, LANES), 1)
    batch = 2

    def frame_copy(j):
        where = (2 * u + j // halves, 2 * (j % halves) + c)
        return remote(tx2.at[j], rx2.at[mine], s2.at[j], r2.at[mine], where)

    def own_frame():
        return pltpu.make_async_copy(tx2.at[e], rx2.at[mine], own_sems.at[2])

    def spectra(step, carry):
        @pl.when((step == 1) & (c == 1) & jnp.logical_not(top))
        def _():
            for slot in range(8, 10):
                arrived(slot)
                widen(slot)

        def one_frame(i, inner):
            f = step * batch + i
            for s in range(stations):
                offset = f * NCHAN + heard[delays_at, 0, s * frames + f]
                row, shift = offset // LANES, offset % LANES
                for r in range(2):
                    parts = [
                        pltpu.roll(
                            series[pl.ds((r * stations + s) * depth + row + q, RADIX_A, stride=QUADS), :],
                            (LANES - shift) % LANES, 1)
                        for q in range(QUADS + 1)
                    ]
                    for q in range(QUADS):
                        cut = jnp.where(lane16 < LANES - shift, parts[q], parts[q + 1])
                        windows[(2 * s + r) * RADIX_A:(2 * s + r + 1) * RADIX_A, q * LANES:(q + 1) * LANES] = cut.astype(BF16)
            passed = jnp.dot(first[...], windows[...], preferred_element_type=F32)
            real, imag = passed[:sk], passed[sk:]
            here = pl.ds(pl.multiple_of(i * sk, sk), sk)
            turned[here, 0:RADIX_B] = (real * twist[0] + imag * twist[1]).astype(BF16)
            turned[here, RADIX_B:] = (imag * twist[0] - real * twist[1]).astype(BF16)
            return inner

        lax.fori_loop(0, batch, one_frame, 0)
        for g in range(QUADS):
            channels = jnp.dot(turned[...], second[:, g * 2 * LANES:(g + 1) * 2 * LANES], preferred_element_type=F32)
            real = channels[:, :LANES].reshape(batch, sk, LANES)
            imag = channels[:, LANES:].reshape(batch, sk, LANES)
            cosine, sine = trig[0, g], trig[1, g]
            turned_re = (real * cosine - imag * sine).reshape(batch * stations, RADIX_A, LANES)
            turned_im = (real * sine + imag * cosine).reshape(batch * stations, RADIX_A, LANES)
            planes[:, g * RADIX_A:(g + 1) * RADIX_A, :] = turned_re
            planes[:, CHAVG + g * RADIX_A:CHAVG + (g + 1) * RADIX_A, :] = turned_im

        def one_out(i, inner):
            def flip(s, deep):
                rows[pl.ds(s, OUTCH, stride=stations), :] = planes[i * stations + s].T
                return deep

            lax.fori_loop(0, stations, flip, 0, unroll=4)
            j = step * batch + i
            tx2[j] = rows[...].astype(BF16).reshape(OUTCH, stations, LANES)

            @pl.when(j == e)
            def _():
                own_frame().start()

            @pl.when(j != e)
            def _():
                frame_copy(j).start()
            return inner

        lax.fori_loop(0, batch, one_out, 0)
        return carry

    lax.fori_loop(0, frames // batch, spectra, 0)

    lane32 = lax.broadcasted_iota(I32, (pairs * stations, LANES), 1)
    half = pairs * stations // 2

    @pl.when(e < frames)
    def _():
        own_frame().wait()

        def get(step, carry):
            g = (mine + step) % pairs
            remote(rx2.at[g], rx2.at[g], s2.at[0], r2.at[g], (tm, pair)).wait_recv()
            return carry

        lax.fori_loop(1, pairs, get, 0)

        def gram(o, carry):
            row = o % 2 * (OUTCH // 2) + o // 2
            left = jnp.concatenate([rx2[g, row].astype(F32) for g in range(pairs)], 0)
            swapped = pltpu.roll(left, CHAVG, 1)
            swapped = jnp.where(lane32 < CHAVG, -swapped, swapped)
            both = jnp.concatenate([left, swapped], 0).astype(BF16)
            right = jnp.concatenate([both, both], 0)
            made = lax.dot_general(left.astype(BF16), right, (((1,), (1,)), ((), ())), preferred_element_type=F32)
            gs[pl.ds(o, half, stride=OUTCH), :] = jnp.where(lane32[:half] < CHAVG, made[:half], made[half:])
            return carry

        lax.fori_loop(0, OUTCH, gram, 0, unroll=4)

        def turn(i, carry):
            block = gs[pl.ds(pl.multiple_of(i * OUTCH, OUTCH), OUTCH), :].T * (1.0 / CHAVG)
            for upper in range(2):
                row = i + half * upper
                a, p = row // GROUP_ST, row % GROUP_ST
                for ri in range(2):
                    for b in range(NGRP):
                        top_row = upper * CHAVG + ri * 32 + b * GROUP_ST
                        tscr[pl.ds(p * 256 + ri * 128 + a * NGRP + b, GROUP_ST, stride=NBLK), :] = block[top_row:top_row + GROUP_ST]
            return carry

        lax.fori_loop(0, half, turn, 0)

        def pack(i, carry):
            p, ri = i // 2, i % 2
            held = tscr[pl.ds(pl.multiple_of(i * 128, 128), 128), :].astype(BF16).reshape(GROUP_ST, NBLK, LANES)
            tx3[pl.ds(p % 4 * GROUP_ST, GROUP_ST), p // 4 * 2 + ri] = held
            return carry

        lax.fori_loop(0, 2 * GROUP_ST, pack, 0)
        frame = tm // 2 * 2 * frames + c * frames + e

        def send(step, carry):
            d = (me + step) % SLICES

            @pl.when(d != me)
            def _():
                remote(tx3.at[d], rx3.at[frame], s3.at[d], r3.at[frame], place_of(d)).start()

            @pl.when(d == me)
            def _():
                pltpu.make_async_copy(tx3.at[d], rx3.at[frame], own_sems.at[3]).start()
            return carry

        lax.fori_loop(0, SLICES, send, 0)

    tell.wait()

    @pl.when(me < SLICES)
    def _():
        def get(f, carry):
            layer, core, j = f // (2 * frames), f // frames % 2, f % frames
            source = (2 * layer + j // halves) * pairs + 2 * (j % halves) + core

            @pl.when(source != me)
            def _():
                remote(rx3.at[f], rx3.at[f], s3.at[0], r3.at[f], (tm, pair)).wait_recv()

            @pl.when(source == me)
            def _():
                pltpu.make_async_copy(tx3.at[0], rx3.at[f], own_sems.at[3]).wait()
            return carry

        lax.fori_loop(0, all_frames, get, 0)
        sums[all_frames] = jnp.zeros((4 * NBLK, LANES), F32)

        def add(f, carry):
            sums[f] = sums[orders[f, 0]] + rx3[f].reshape(4 * NBLK, LANES).astype(F32)
            return carry

        lax.fori_loop(0, all_frames, add, 0)

        def gather(b, carry):
            binned[pl.ds(pl.multiple_of(b * 4 * NBLK, 4 * NBLK), 4 * NBLK), :] = sums[orders[all_frames + b, 0]]
            return carry

        lax.fori_loop(0, BINS, gather, 0)

        def choose(i, carry):
            q, k = i // slots, i % slots
            block = heard[q, 0, (stations + 1) * frames + k]
            held = binned[pl.ds(block, BINS * 4, stride=NBLK), :]
            tx4[:, q, k] = held.astype(BF16).reshape(owners, piece, LANES)
            return carry

        lax.fori_loop(0, pairs * slots, choose, 0)

        def send(step, carry):
            d = (me + step) % devices
            remote(tx4.at[d // pairs, d % pairs], rx4.at[me], s4.at[d], r4.at[me], place_of(d)).start()
            return carry

        lax.fori_loop(1, devices, send, 0)
        pltpu.make_async_copy(tx4.at[tm, pair], rx4.at[me], own_sems.at[4]).start()

    @pl.when(me < SLICES)
    def _():
        pltpu.make_async_copy(tx4.at[tm, pair], rx4.at[me], own_sems.at[4]).wait()

    def collect(d, carry):
        @pl.when(d != me)
        def _():
            remote(rx4.at[d], rx4.at[d], s4.at[0], r4.at[d], (tm, pair)).wait_recv()
        return carry

    lax.fori_loop(0, SLICES, collect, 0)
    landed[...] = rx4[...].reshape(landed.shape).astype(F32)
    for b in range(bins_here):
        for k in range(slots):
            for part in range(2):
                for ri in range(2):
                    held = landed[pl.ds(k * piece + b * 4 + part * 2 + ri, SLICES, stride=slots * piece), :]
                    out[b, k, ri, part * SLICES:(part + 1) * SLICES, :] = held

    def small_sent(step, carry):
        small_copy(step, (me + step) % devices, me).wait_send()
        return carry

    lax.fori_loop(1, devices, small_sent, 0)

    def sent(index):
        sample_copy(index, rxu.at[0], at(u, h, c), 0).wait_send()

    @pl.when(is00)
    def _():
        for index in range(8, 12):
            sent(index)

        @pl.when(below)
        def _():
            for index in range(6):
                sent(index)

        @pl.when(jnp.logical_not(top))
        def _():
            for index in range(12, 14):
                sent(index)

    @pl.when(is10)
    def _():
        for index in range(4):
            sent(index)

        @pl.when(below)
        def _():
            for index in range(4, 8):
                sent(index)

        @pl.when(jnp.logical_not(top))
        def _():
            for index in range(8, 10):
                sent(index)

    @pl.when(c == 1)
    def _():
        for index in range(4):
            sent(index)

    @pl.when(is11 & below)
    def _():
        for index in range(4, 6):
            sent(index)

    def frame_sent(j, carry):
        @pl.when(j != e)
        def _():
            frame_copy(j).wait_send()
        return carry

    lax.fori_loop(0, frames, frame_sent, 0)

    @pl.when(e < frames)
    def _():
        def slice_sent(d, carry):
            @pl.when(d != me)
            def _():
                remote(tx3.at[d], rx3.at[0], s3.at[d], r3.at[0], place_of(d)).wait_send()
            return carry

        lax.fori_loop(0, SLICES, slice_sent, 0)

    @pl.when(me < SLICES)
    def _():
        def sum_sent(step, carry):
            d = (me + step) % devices
            remote(tx4.at[d // pairs, d % pairs], rx4.at[me], s4.at[d], r4.at[me], place_of(d)).wait_send()
            return carry

        lax.fori_loop(1, devices, sum_sent, 0)


VMEM = pl.BlockSpec(memory_space=pltpu.VMEM)
SMEM = pl.BlockSpec(memory_space=pltpu.SMEM)
ANY = pl.BlockSpec(memory_space=pl.ANY)


def body(voltages, delays, phase_model, phase_bins, assignment):
    owners, pairs = lax.axis_size("tm"), lax.axis_size("pair")
    devices = owners * pairs
    stations, samples = voltages.shape[1], voltages.shape[2]
    frames = samples // NCHAN
    slots = assignment.shape[0]
    all_frames = owners * frames
    bins_here = BINS // owners
    piece = bins_here * 4
    sk = stations * RADIX_A
    batch = 2

    first, twist, second = section_tables(stations)
    span = (frames + AHEAD) * UNIT
    scratch = [
        pltpu.VMEM((2, LANES), I32),
        pltpu.VMEM(first.shape, BF16),
        pltpu.VMEM(twist.shape, F32),
        pltpu.VMEM(second.shape, BF16),
        pltpu.VMEM((frames + AHEAD, 2, stations, NCHAN), BF16),
        pltpu.VMEM((2 * stations * (span + 8), LANES), F32),
        pltpu.VMEM((2 * sk, RADIX_B), BF16),
        pltpu.VMEM((batch * sk, 2 * RADIX_B), BF16),
        pltpu.VMEM((batch * stations, LANES, LANES), F32),
        pltpu.VMEM((OUTCH * stations, LANES), F32),
        pltpu.VMEM((8, NCHAN), F32),
        pltpu.VMEM((8 * UNIT, LANES), F32),
        pltpu.VMEM((2, QUADS, sk, LANES), F32),
        pltpu.VMEM((frames, OUTCH, stations, LANES), BF16),
        pltpu.VMEM((pairs, OUTCH, stations, LANES), BF16),
        pltpu.VMEM((pairs * stations // 2 * OUTCH, LANES), F32),
        pltpu.VMEM((2 * pairs * stations * pairs * stations, LANES), F32),
        pltpu.VMEM((SLICES, 4, NBLK, LANES), BF16),
        pltpu.VMEM((all_frames, 4, NBLK, LANES), BF16),
        pltpu.VMEM((all_frames + 1, 4 * NBLK, LANES), F32),
        pltpu.VMEM((BINS * 4 * NBLK, LANES), F32),
        pltpu.VMEM((owners, pairs, slots, piece, LANES), BF16),
        pltpu.VMEM((SLICES, slots, piece, LANES), BF16),
        pltpu.VMEM((SLICES * slots * piece, LANES), F32),
        pltpu.VMEM((devices, 2, LANES), I32),
        pltpu.SMEM((devices, 2, LANES), I32),
        pltpu.VMEM((all_frames + BINS, LANES), I32),
        pltpu.SMEM((all_frames + BINS, LANES), I32),
        pltpu.SemaphoreType.DMA((4,)),
        pltpu.SemaphoreType.DMA((devices,)),
        pltpu.SemaphoreType.DMA((devices,)),
        pltpu.SemaphoreType.DMA((14,)),
        pltpu.SemaphoreType.DMA((frames + AHEAD,)),
        pltpu.SemaphoreType.DMA((frames,)),
        pltpu.SemaphoreType.DMA((pairs,)),
        pltpu.SemaphoreType.DMA((SLICES,)),
        pltpu.SemaphoreType.DMA((all_frames,)),
        pltpu.SemaphoreType.DMA((devices,)),
        pltpu.SemaphoreType.DMA((SLICES,)),
        pltpu.SemaphoreType.DMA((6,)),
        pltpu.SemaphoreType.DMA((4,)),
    ]
    return pl.pallas_call(
        functools.partial(fused_kernel, (owners, pairs, frames, stations, slots)),
        out_shape=jax.ShapeDtypeStruct((bins_here, slots, 2, GROUP_ST * GROUP_ST, OUTCH), F32),
        in_specs=[SMEM, SMEM, SMEM, ANY, ANY, ANY, ANY, ANY],
        out_specs=VMEM,
        scratch_shapes=scratch,
        compiler_params=pltpu.CompilerParams(
            collective_id=0, has_side_effects=True, vmem_limit_bytes=56 * 1024 * 1024),
        name="correlate",
    )(delays, phase_bins, assignment, voltages, phase_model, first, twist, second)


def solution(mesh):
    in_specs = (P(None, "pair", "tm"), P("pair", "tm"), P(), P("tm"), P("pair"))
    out_specs = P("tm", "pair", None, None, None)
    return jax.shard_map(body, mesh=mesh, in_specs=in_specs, out_specs=out_specs, check_vma=False)
```

time: 111 us -> 83.7 us (0.75)
  the two profiles are of different devices: /device:TPU:0 before, /device:TPU:11 now
where the time goes in v1:
time: 83.7 us; the launch traced here: 83.5 us
  Pallas kernels  79.8 us (95%)
  local copies, waits for them, and re-layouts  3.65 us (4%)
    pallas_call x1, Pallas kernels, body(): pl.pallas_call(functools.partial(fused_kernel, (owners, pairs, frames, st...  79.8 us
    unnamed x2, local copies, waits for them, and re-layouts  3.65 us

profile of v1, /device:TPU:11, one launch (start us, length us, event | category | flops | bytes accessed | tf_op | source)
XLA Modules:
  0.0 83.5 jit_solution(12589325842736932180)
XLA Ops:
  0.0 1.3 %copy.9.delays = s32[8,4]{1,0:T(8,128)} copy(s32[8,4]{0,1:T(4,128)} %param.9) | data formatting | bytes 256 | tf_op args[1]
  1.3 79.8 %correlate.1 = f32[4,4,2,64,128]{4,3,2,1,0:T(8,128)} custom-call(s32[8,4]{1,0:T(8,128)} %copy.9.delays, s32[4]{0:T(128)} %phase_bins.1, s32[4]{0:T(128)} %assignment.1, bf16[2,8,32768]{2,1,0:T(8,128)(2,1)} %voltages.1, f32[32,8192]{1,0:T(8,128)} %phase_model.1, bf16[256,256]{1,0:T(8,128)(2,1)} %constant.6.clone.first_hbm, ...), custom_call_target="tpu_custom_call" | custom-call | tf_op jit(solution)/shard_map/correlate/pallas_call | solution.py:667
  81.2 2.3 %copy.11 = f32[4,4,2,64,128]{4,3,2,1,0:T(8,128)} copy(f32[4,4,2,64,128]{4,3,2,1,0:T(8,128)} %correlate.1) | data formatting | bytes 2097152

commit v2 on v1

--- a/solution.py
+++ b/solution.py
@@ -69,20 +69,19 @@
 
 def fused_kernel(dims, delays, phase_bins, assignment, voltages, phase_model, first_hbm, twist_hbm, second_hbm, out,
                  small, first, twist, second, rxu, series, windows, turned, planes, rows, phases, phase_rows, trig,
-                 tx2, rx2, gs, tscr, tx3, rx3, sums, binned, tx4, rx4, landed, rx0, heard, tables, orders,
-                 load_sems, s0, r0, s1, r1, s2, r2, s3, r3, s4, r4, own_sems, unit_sems):
+                 tx2, rx2, gs, tscr, tx3, rx3, sums, tx4, rx4, landed, rxd, rxb, heard, tables, orders,
+                 load_sems, s0, r0, s1, r1, s2, r2, s3, r3, s4, r4, s5, own_sems, unit_sems):
     owners, pairs, frames, stations, slots = dims
     devices, layers, halves = owners * pairs, owners // 2, pairs // 2
     all_frames = owners * frames
     bins_here = BINS // owners
-    piece = bins_here * 4
     sk = stations * RADIX_A
     depth = (frames + AHEAD) * UNIT + 8
     tm, pair = lax.axis_index("tm"), lax.axis_index("pair")
     u, h, m, c = tm // 2, tm % 2, pair // 2, pair % 2
     me = tm * pairs + pair
     mine = 2 * m + h
-    e = h * halves + m
+    e = jnp.where(m < 2, (h + m) % 2 * 2 + m, frames)
     top = u == layers - 1
 
     def place_of(device):
@@ -105,14 +104,11 @@
     lane = lax.broadcasted_iota(I32, (1, LANES), 1)
     listed, marked = jnp.zeros((1, LANES), I32), jnp.zeros((1, LANES), I32)
     for i in range(stations * frames):
-        listed = jnp.where(lane == i, delays[i // frames, i % frames], listed)
+        listed = jnp.where(lane == i, delays[i // stations, i % stations], listed)
     for i in range(frames):
-        listed = jnp.where(lane == stations * frames + i, phase_bins[i], listed)
         marked = jnp.where(lane == tm * frames + i, phase_bins[i] + 1, marked)
-    for i in range(slots):
-        listed = jnp.where(lane == (stations + 1) * frames + i, assignment[i], listed)
-    small[0:1] = listed
-    small[1:2] = marked
+    small[0] = listed
+    small[1] = marked
 
     barrier = pltpu.get_barrier_semaphore()
 
@@ -120,19 +116,30 @@
         pl.semaphore_signal(barrier, inc=1, device_id=place_of((me + step) % devices), device_id_type=MESH)
         return carry
 
-    lax.fori_loop(1, devices, greet, 0)
+    lax.fori_loop(1, devices, greet, 0, unroll=True) if devices < 64 else lax.fori_loop(1, devices, greet, 0)
     pl.semaphore_wait(barrier, devices - 1)
 
-    def small_copy(step, peer, slot):
-        return remote(small, rx0.at[slot], s0.at[step], r0.at[slot], place_of(peer))
-
-    def start_small(step, carry):
-        small_copy(step, (me + step) % devices, me).start()
-        return carry
-
-    lax.fori_loop(1, devices, start_small, 0)
-    own_small = pltpu.make_async_copy(small, rx0.at[me], own_sems.at[0])
-    own_small.start()
+    def delay_copy():
+        return remote(small.at[0], rxd, s0.at[0], r0.at[0], (2 * u + c, 2 * m + h))
+
+    def own_delays():
+        return pltpu.make_async_copy(small.at[0], rxd, own_sems.at[0])
+
+    @pl.when(c == h)
+    def _():
+        own_delays().start()
+
+    @pl.when(c != h)
+    def _():
+        delay_copy().start()
+
+    def start_bins(step, carry):
+        remote(small.at[1], rxb.at[tm], s0.at[1], r0.at[1], ((tm + step) % owners, pair)).start()
+        return carry
+
+    lax.fori_loop(1, owners, start_bins, 0)
+    own_bins = pltpu.make_async_copy(small.at[1], rxb.at[tm], own_sems.at[5])
+    own_bins.start()
 
     def at(layer, half, core):
         return (2 * layer + half, 2 * m + core)
@@ -204,34 +211,17 @@
 
     lax.fori_loop(0, stations, one_phase, 0)
 
-    own_small.wait()
-
-    def finish_small(step, carry):
-        source = (me + devices - step) % devices
-        small_copy(step, source, source).wait_recv()
-        return carry
-
-    lax.fori_loop(1, devices, finish_small, 0)
-    hear = pltpu.make_async_copy(rx0, heard, own_sems.at[1])
+    @pl.when(c == h)
+    def _():
+        own_delays().wait()
+
+    @pl.when(c != h)
+    def _():
+        delay_copy().wait_recv()
+
+    hear = pltpu.make_async_copy(rxd, heard, own_sems.at[1])
     hear.start()
     hear.wait()
-    delays_at = ((2 * u + c) * pairs + 2 * m + h)
-
-    line = rx0[0, 1:2, :]
-    for t in range(1, owners):
-        line = line + rx0[t * pairs, 1:2, :]
-    span = jnp.broadcast_to(line, (all_frames, LANES))
-    across = lax.broadcasted_iota(I32, (all_frames, LANES), 1)
-    down = lax.broadcasted_iota(I32, (all_frames, LANES), 0)
-    column = jnp.max(jnp.where(across == down, span, 0), 1, keepdims=True)
-    found = jnp.max(jnp.where((span == column) & (across < down), across, -1), 1, keepdims=True)
-    tables[0:all_frames] = jnp.broadcast_to(jnp.where(found < 0, all_frames, found), (all_frames, LANES))
-    down = lax.broadcasted_iota(I32, (BINS, LANES), 0)
-    across = lax.broadcasted_iota(I32, (BINS, LANES), 1)
-    found = jnp.max(jnp.where(jnp.broadcast_to(line, (BINS, LANES)) == down + 1, across, -1), 1, keepdims=True)
-    tables[all_frames:] = jnp.broadcast_to(jnp.where(found < 0, all_frames, found), (BINS, LANES))
-    tell = pltpu.make_async_copy(tables, orders, own_sems.at[5])
-    tell.start()
 
     def widen(slot):
         def one(j, carry):
@@ -239,7 +229,7 @@
                 held = rxu[slot, r, :, pl.ds(pl.multiple_of(j * LANES, LANES), LANES)].astype(F32)
                 series[pl.ds(r * stations * depth + slot * UNIT + j, stations, stride=depth), :] = held
             return carry
-        lax.fori_loop(0, UNIT, one, 0, unroll=4)
+        lax.fori_loop(0, UNIT, one, 0, unroll=8)
 
     def blank(slot):
         def one(i, carry):
@@ -325,11 +315,10 @@
     batch = 2
 
     def frame_copy(j):
-        where = (2 * u + j // halves, 2 * (j % halves) + c)
-        return remote(tx2.at[j], rx2.at[mine], s2.at[j], r2.at[mine], where)
+        return remote(tx2.at[j], rx2.at[mine], s2.at[0], r2.at[0], (2 * u + (j + 1) // 2 % 2, j % 2 * 2 + c))
 
     def own_frame():
-        return pltpu.make_async_copy(tx2.at[e], rx2.at[mine], own_sems.at[2])
+        return pltpu.make_async_copy(tx2.at[e], rx2.at[mine], own_sems.at[6])
 
     def spectra(step, carry):
         @pl.when((step == 1) & (c == 1) & jnp.logical_not(top))
@@ -341,7 +330,7 @@
         def one_frame(i, inner):
             f = step * batch + i
             for s in range(stations):
-                offset = f * NCHAN + heard[delays_at, 0, s * frames + f]
+                offset = f * NCHAN + heard[0, f * stations + s]
                 row, shift = offset // LANES, offset % LANES
                 for r in range(2):
                     parts = [
@@ -394,6 +383,25 @@
 
     lax.fori_loop(0, frames // batch, spectra, 0)
 
+    own_bins.wait()
+    rest = rxb.at[pl.ds(0, owners - 1)]
+    remote(rest, rest, s0.at[1], r0.at[1], (tm, pair)).wait_recv()
+    line = rxb[0]
+    for t in range(1, owners):
+        line = line + rxb[t]
+    span = jnp.broadcast_to(line, (all_frames, LANES))
+    across = lax.broadcasted_iota(I32, (all_frames, LANES), 1)
+    down = lax.broadcasted_iota(I32, (all_frames, LANES), 0)
+    column = jnp.max(jnp.where(across == down, span, 0), 1, keepdims=True)
+    found = jnp.max(jnp.where((span == column) & (across < down), across, -1), 1, keepdims=True)
+    tables[0:all_frames] = jnp.broadcast_to(jnp.where(found < 0, all_frames, found), (all_frames, LANES))
+    down = lax.broadcasted_iota(I32, (BINS, LANES), 0)
+    across = lax.broadcasted_iota(I32, (BINS, LANES), 1)
+    found = jnp.max(jnp.where(jnp.broadcast_to(line, (BINS, LANES)) == down + 1, across, -1), 1, keepdims=True)
+    tables[all_frames:] = jnp.broadcast_to(jnp.where(found < 0, all_frames, found), (BINS, LANES))
+    tell = pltpu.make_async_copy(tables, orders, own_sems.at[2])
+    tell.start()
+
     lane32 = lax.broadcasted_iota(I32, (pairs * stations, LANES), 1)
     half = pairs * stations // 2
 
@@ -401,12 +409,8 @@
     def _():
         own_frame().wait()
 
-        def get(step, carry):
-            g = (mine + step) % pairs
-            remote(rx2.at[g], rx2.at[g], s2.at[0], r2.at[g], (tm, pair)).wait_recv()
-            return carry
-
-        lax.fori_loop(1, pairs, get, 0)
+        rest = rx2.at[pl.ds(0, pairs - 1)]
+        remote(rest, rest, s2.at[0], r2.at[0], (tm, pair)).wait_recv()
 
         def gram(o, carry):
             row = o % 2 * (OUTCH // 2) + o // 2
@@ -419,7 +423,7 @@
             gs[pl.ds(o, half, stride=OUTCH), :] = jnp.where(lane32[:half] < CHAVG, made[:half], made[half:])
             return carry
 
-        lax.fori_loop(0, OUTCH, gram, 0, unroll=4)
+        lax.fori_loop(0, OUTCH, gram, 0, unroll=16)
 
         def turn(i, carry):
             block = gs[pl.ds(pl.multiple_of(i * OUTCH, OUTCH), OUTCH), :].T * (1.0 / CHAVG)
@@ -432,15 +436,19 @@
                         tscr[pl.ds(p * 256 + ri * 128 + a * NGRP + b, GROUP_ST, stride=NBLK), :] = block[top_row:top_row + GROUP_ST]
             return carry
 
-        lax.fori_loop(0, half, turn, 0)
-
-        def pack(i, carry):
-            p, ri = i // 2, i % 2
-            held = tscr[pl.ds(pl.multiple_of(i * 128, 128), 128), :].astype(BF16).reshape(GROUP_ST, NBLK, LANES)
-            tx3[pl.ds(p % 4 * GROUP_ST, GROUP_ST), p // 4 * 2 + ri] = held
-            return carry
-
-        lax.fori_loop(0, 2 * GROUP_ST, pack, 0)
+        lax.fori_loop(0, half, turn, 0, unroll=4)
+
+        def pack(p, carry):
+            real = tscr[pl.ds(pl.multiple_of(p * 256, 256), 128), :].reshape(GROUP_ST, NBLK, LANES)
+            imag = tscr[pl.ds(pl.multiple_of(p * 256 + 128, 128), 128), :].reshape(GROUP_ST, NBLK, LANES)
+            q = lax.broadcasted_iota(I32, (GROUP_ST, NBLK, LANES), 0)
+            ab = lax.broadcasted_iota(I32, (GROUP_ST, NBLK, LANES), 1)
+            a, b = ab // NGRP, ab % NGRP
+            upper = (a < b) | ((a == b) & (p <= q))
+            tx3[pl.ds(p % 4 * GROUP_ST, GROUP_ST), p // 4] = jnp.where(upper, real, imag).astype(BF16)
+            return carry
+
+        lax.fori_loop(0, GROUP_ST, pack, 0, unroll=2)
         frame = tm // 2 * 2 * frames + c * frames + e
 
         def send(step, carry):
@@ -448,88 +456,142 @@
 
             @pl.when(d != me)
             def _():
-                remote(tx3.at[d], rx3.at[frame], s3.at[d], r3.at[frame], place_of(d)).start()
+                remote(tx3.at[d], rx3.at[frame], s3.at[0], r3.at[0], place_of(d)).start()
 
             @pl.when(d == me)
             def _():
                 pltpu.make_async_copy(tx3.at[d], rx3.at[frame], own_sems.at[3]).start()
             return carry
 
-        lax.fori_loop(0, SLICES, send, 0)
+        lax.fori_loop(0, SLICES, send, 0, unroll=4)
 
     tell.wait()
 
     @pl.when(me < SLICES)
     def _():
-        def get(f, carry):
-            layer, core, j = f // (2 * frames), f // frames % 2, f % frames
-            source = (2 * layer + j // halves) * pairs + 2 * (j % halves) + core
-
-            @pl.when(source != me)
-            def _():
-                remote(rx3.at[f], rx3.at[f], s3.at[0], r3.at[f], (tm, pair)).wait_recv()
-
-            @pl.when(source == me)
-            def _():
-                pltpu.make_async_copy(tx3.at[0], rx3.at[f], own_sems.at[3]).wait()
-            return carry
-
-        lax.fori_loop(0, all_frames, get, 0)
-        sums[all_frames] = jnp.zeros((4 * NBLK, LANES), F32)
+        @pl.when(e < frames)
+        def _():
+            pltpu.make_async_copy(tx3.at[0], rx3.at[0], own_sems.at[3]).wait()
+            rest = rx3.at[pl.ds(0, all_frames - 1)]
+            remote(rest, rest, s3.at[0], r3.at[0], (tm, pair)).wait_recv()
+
+        @pl.when(e >= frames)
+        def _():
+            remote(rx3, rx3, s3.at[0], r3.at[0], (tm, pair)).wait_recv()
+
+        sums[all_frames] = jnp.zeros((2 * NBLK, LANES), F32)
 
         def add(f, carry):
-            sums[f] = sums[orders[f, 0]] + rx3[f].reshape(4 * NBLK, LANES).astype(F32)
+            sums[f] = sums[orders[f, 0]] + rx3[f].reshape(2 * NBLK, LANES).astype(F32)
             return carry
 
         lax.fori_loop(0, all_frames, add, 0)
 
         def gather(b, carry):
-            binned[pl.ds(pl.multiple_of(b * 4 * NBLK, 4 * NBLK), 4 * NBLK), :] = sums[orders[all_frames + b, 0]]
-            return carry
-
-        lax.fori_loop(0, BINS, gather, 0)
-
-        def choose(i, carry):
-            q, k = i // slots, i % slots
-            block = heard[q, 0, (stations + 1) * frames + k]
-            held = binned[pl.ds(block, BINS * 4, stride=NBLK), :]
-            tx4[:, q, k] = held.astype(BF16).reshape(owners, piece, LANES)
-            return carry
-
-        lax.fori_loop(0, pairs * slots, choose, 0)
+            held = sums[orders[all_frames + b, 0]].astype(BF16)
+            tx4[b // bins_here, pl.ds(pl.multiple_of(b % bins_here * 2 * NBLK, 2 * NBLK), 2 * NBLK), :] = held
+            return carry
+
+        lax.fori_loop(0, BINS, gather, 0, unroll=8)
 
         def send(step, carry):
-            d = (me + step) % devices
-            remote(tx4.at[d // pairs, d % pairs], rx4.at[me], s4.at[d], r4.at[me], place_of(d)).start()
-            return carry
-
-        lax.fori_loop(1, devices, send, 0)
-        pltpu.make_async_copy(tx4.at[tm, pair], rx4.at[me], own_sems.at[4]).start()
-
-    @pl.when(me < SLICES)
-    def _():
-        pltpu.make_async_copy(tx4.at[tm, pair], rx4.at[me], own_sems.at[4]).wait()
-
-    def collect(d, carry):
+            t = (tm + step) % owners
+            remote(tx4.at[t], rx4.at[me], s4.at[0], r4.at[me], (t, pair)).start()
+            return carry
+
+        lax.fori_loop(1, owners, send, 0)
+        pltpu.make_async_copy(tx4.at[tm], rx4.at[me], own_sems.at[4]).start()
+
+    sources = SLICES // pairs
+
+    def pass_on(d, other):
+        return remote(rx4.at[d], rx4.at[d], s5.at[0], r4.at[d], (tm, other))
+
+    def landing(d):
+        def one(i, carry):
+            held = rx4[d, pl.ds(pl.multiple_of(i * NBLK, NBLK), NBLK), :].astype(F32)
+            landed[pl.ds(i // 2 * NBLK * 2 * SLICES + i % 2 * SLICES + d, NBLK, stride=2 * SLICES), :] = held
+            return carry
+
+        lax.fori_loop(0, 2 * bins_here, one, 0, unroll=2 * bins_here)
+
+    def nearest(step):
+        if sources != 8:
+            return (tm + step) % sources
+        return (tm + step) % 2 + (tm // 2 + step // 2) % 2 * 2 + (tm // 4 + step // 4) % 2 * 4
+
+    def first_hop(step, carry):
+        i = nearest(step)
+        d = i * pairs + pair
+
+        @pl.when(d == me)
+        def _():
+            pltpu.make_async_copy(tx4.at[tm], rx4.at[d], own_sems.at[4]).wait()
+
         @pl.when(d != me)
         def _():
             remote(rx4.at[d], rx4.at[d], s4.at[0], r4.at[d], (tm, pair)).wait_recv()
-        return carry
-
-    lax.fori_loop(0, SLICES, collect, 0)
-    landed[...] = rx4[...].reshape(landed.shape).astype(F32)
-    for b in range(bins_here):
+
+        for n in range(1, halves):
+            pass_on(d, (pair + 2 * n) % pairs).start()
+        pass_on(d, pair + 1 - 2 * c).start()
+        landing(d)
+        return carry
+
+    lax.fori_loop(0, sources, first_hop, 0)
+
+    def second_hop(step, carry):
+        i = nearest(step)
+        for n in range(1, halves):
+            d = i * pairs + (pair + 2 * n) % pairs
+            remote(rx4.at[d], rx4.at[d], s4.at[0], r4.at[d], (tm, pair)).wait_recv()
+            pass_on(d, pair + 1 - 2 * c).start()
+            landing(d)
+        return carry
+
+    lax.fori_loop(0, sources, second_hop, 0)
+
+    def third_hop(step, carry):
+        i = nearest(step)
+        for n in range(halves):
+            d = i * pairs + (pair + 1 - 2 * c + 2 * n) % pairs
+            remote(rx4.at[d], rx4.at[d], s4.at[0], r4.at[d], (tm, pair)).wait_recv()
+            landing(d)
+        return carry
+
+    lax.fori_loop(0, sources, third_hop, 0)
+
+    place = lax.broadcasted_iota(I32, (GROUP_ST, LANES), 0)
+    none = jnp.zeros((GROUP_ST, LANES), I32)
+    span = 2 * SLICES
+
+    def one_bin(b, carry):
         for k in range(slots):
-            for part in range(2):
-                for ri in range(2):
-                    held = landed[pl.ds(k * piece + b * 4 + part * 2 + ri, SLICES, stride=slots * piece), :]
-                    out[b, k, ri, part * SLICES:(part + 1) * SLICES, :] = held
-
-    def small_sent(step, carry):
-        small_copy(step, (me + step) % devices, me).wait_send()
-        return carry
-
-    lax.fori_loop(1, devices, small_sent, 0)
+            block = assignment[k]
+            a, bb = block // NGRP, block % NGRP
+            row, column = none + a, none + bb
+            ahead, within = row < column, row == column
+            here = (b * NBLK + block) * span
+            there = (b * NBLK + bb * NGRP + a) * span
+            for p in range(GROUP_ST):
+                straight = landed[pl.ds(here + p * GROUP_ST, GROUP_ST), :]
+                mirrored = landed[pl.ds(there + p, GROUP_ST, stride=GROUP_ST), :]
+                upper = ahead | (within & (place >= p))
+                real = jnp.where(upper, straight, mirrored)
+                imag = jnp.where(upper, -mirrored, straight)
+                imag = jnp.where(within & (place == p), 0.0, imag)
+                out[b, k, 0, p * GROUP_ST:(p + 1) * GROUP_ST, :] = real.astype(BF16)
+                out[b, k, 1, p * GROUP_ST:(p + 1) * GROUP_ST, :] = imag.astype(BF16)
+        return carry
+
+    lax.fori_loop(0, bins_here, one_bin, 0)
+
+    rest = rxb.at[pl.ds(0, owners - 1)]
+    remote(rest, rest, s0.at[1], r0.at[1], (tm, pair)).wait_send()
+
+    @pl.when(c != h)
+    def _():
+        delay_copy().wait_send()
 
     def sent(index):
         sample_copy(index, rxu.at[0], at(u, h, c), 0).wait_send()
@@ -574,32 +636,31 @@
         for index in range(4, 6):
             sent(index)
 
-    def frame_sent(j, carry):
-        @pl.when(j != e)
-        def _():
-            frame_copy(j).wait_send()
-        return carry
-
-    lax.fori_loop(0, frames, frame_sent, 0)
+    def all_sent(ref, count, sem):
+        rest = ref.at[pl.ds(0, count)]
+        remote(rest, rest, sem, r4.at[0], (tm, pair)).wait_send()
 
     @pl.when(e < frames)
     def _():
-        def slice_sent(d, carry):
-            @pl.when(d != me)
-            def _():
-                remote(tx3.at[d], rx3.at[0], s3.at[d], r3.at[0], place_of(d)).wait_send()
-            return carry
-
-        lax.fori_loop(0, SLICES, slice_sent, 0)
+        all_sent(tx2, frames - 1, s2.at[0])
+
+        @pl.when(me < SLICES)
+        def _():
+            all_sent(tx3, SLICES - 1, s3.at[0])
+
+        @pl.when(me >= SLICES)
+        def _():
+            all_sent(tx3, SLICES, s3.at[0])
+
+    @pl.when(e >= frames)
+    def _():
+        all_sent(tx2, frames, s2.at[0])
 
     @pl.when(me < SLICES)
     def _():
-        def sum_sent(step, carry):
-            d = (me + step) % devices
-            remote(tx4.at[d // pairs, d % pairs], rx4.at[me], s4.at[d], r4.at[me], place_of(d)).wait_send()
-            return carry
-
-        lax.fori_loop(1, devices, sum_sent, 0)
+        all_sent(tx4, owners - 1, s4.at[0])
+
+    all_sent(rx4, sources * (2 * halves - 1), s5.at[0])
 
 
 VMEM = pl.BlockSpec(memory_space=pltpu.VMEM)
@@ -615,14 +676,13 @@
     slots = assignment.shape[0]
     all_frames = owners * frames
     bins_here = BINS // owners
-    piece = bins_here * 4
     sk = stations * RADIX_A
     batch = 2
 
     first, twist, second = section_tables(stations)
     span = (frames + AHEAD) * UNIT
     scratch = [
-        pltpu.VMEM((2, LANES), I32),
+        pltpu.VMEM((2, 1, LANES), I32),
         pltpu.VMEM(first.shape, BF16),
         pltpu.VMEM(twist.shape, F32),
         pltpu.VMEM(second.shape, BF16),
@@ -639,41 +699,43 @@
         pltpu.VMEM((pairs, OUTCH, stations, LANES), BF16),
         pltpu.VMEM((pairs * stations // 2 * OUTCH, LANES), F32),
         pltpu.VMEM((2 * pairs * stations * pairs * stations, LANES), F32),
-        pltpu.VMEM((SLICES, 4, NBLK, LANES), BF16),
-        pltpu.VMEM((all_frames, 4, NBLK, LANES), BF16),
-        pltpu.VMEM((all_frames + 1, 4 * NBLK, LANES), F32),
-        pltpu.VMEM((BINS * 4 * NBLK, LANES), F32),
-        pltpu.VMEM((owners, pairs, slots, piece, LANES), BF16),
-        pltpu.VMEM((SLICES, slots, piece, LANES), BF16),
-        pltpu.VMEM((SLICES * slots * piece, LANES), F32),
-        pltpu.VMEM((devices, 2, LANES), I32),
-        pltpu.SMEM((devices, 2, LANES), I32),
+        pltpu.VMEM((SLICES, 2, NBLK, LANES), BF16),
+        pltpu.VMEM((all_frames, 2, NBLK, LANES), BF16),
+        pltpu.VMEM((all_frames + 1, 2 * NBLK, LANES), F32),
+        pltpu.VMEM((owners, bins_here * 2 * NBLK, LANES), BF16),
+        pltpu.VMEM((SLICES, bins_here * 2 * NBLK, LANES), BF16),
+        pltpu.VMEM((bins_here * NBLK * 2 * SLICES, LANES), F32),
+        pltpu.VMEM((1, LANES), I32),
+        pltpu.VMEM((owners, 1, LANES), I32),
+        pltpu.SMEM((1, LANES), I32),
         pltpu.VMEM((all_frames + BINS, LANES), I32),
         pltpu.SMEM((all_frames + BINS, LANES), I32),
         pltpu.SemaphoreType.DMA((4,)),
-        pltpu.SemaphoreType.DMA((devices,)),
-        pltpu.SemaphoreType.DMA((devices,)),
+        pltpu.SemaphoreType.DMA((2,)),
+        pltpu.SemaphoreType.DMA((2,)),
         pltpu.SemaphoreType.DMA((14,)),
         pltpu.SemaphoreType.DMA((frames + AHEAD,)),
-        pltpu.SemaphoreType.DMA((frames,)),
-        pltpu.SemaphoreType.DMA((pairs,)),
+        pltpu.SemaphoreType.DMA((1,)),
+        pltpu.SemaphoreType.DMA((1,)),
+        pltpu.SemaphoreType.DMA((1,)),
+        pltpu.SemaphoreType.DMA((1,)),
+        pltpu.SemaphoreType.DMA((1,)),
         pltpu.SemaphoreType.DMA((SLICES,)),
-        pltpu.SemaphoreType.DMA((all_frames,)),
-        pltpu.SemaphoreType.DMA((devices,)),
-        pltpu.SemaphoreType.DMA((SLICES,)),
-        pltpu.SemaphoreType.DMA((6,)),
+        pltpu.SemaphoreType.DMA((1,)),
+        pltpu.SemaphoreType.DMA((7,)),
         pltpu.SemaphoreType.DMA((4,)),
     ]
-    return pl.pallas_call(
+    result = pl.pallas_call(
         functools.partial(fused_kernel, (owners, pairs, frames, stations, slots)),
-        out_shape=jax.ShapeDtypeStruct((bins_here, slots, 2, GROUP_ST * GROUP_ST, OUTCH), F32),
+        out_shape=pltpu.VMEM((bins_here, slots, 2, GROUP_ST * GROUP_ST, OUTCH), BF16),
         in_specs=[SMEM, SMEM, SMEM, ANY, ANY, ANY, ANY, ANY],
         out_specs=VMEM,
         scratch_shapes=scratch,
         compiler_params=pltpu.CompilerParams(
             collective_id=0, has_side_effects=True, vmem_limit_bytes=56 * 1024 * 1024),
         name="correlate",
-    )(delays, phase_bins, assignment, voltages, phase_model, first, twist, second)
+    )(delays.T, phase_bins, assignment, voltages, phase_model, first, twist, second)
+    return result.astype(F32)
 
 
 def solution(mesh):

time: 83.7 us -> 66.6 us (0.80)
  the two profiles are of different devices: /device:TPU:11 before, /device:TPU:0 now
where the time goes in v2:
time: 66.6 us; the launch traced here: 66.4 us
  Pallas kernels  65.3 us (98%)
  other arithmetic  1.09 us (2%)
    pallas_call x1, Pallas kernels, body(): pl.pallas_call(functools.partial(fused_kernel, (owners, pairs, frames, st...  65.3 us

profile of v2, /device:TPU:0, one launch (start us, length us, event | category | flops | bytes accessed | tf_op | source)
XLA Modules:
  0.0 66.4 jit_solution(11455064817114960838)
XLA Ops:
  0.0 65.3 %correlate.1 = bf16[4,4,2,64,128]{4,3,2,1,0:T(8,128)(2,1)S(1)} custom-call(s32[4,8]{1,0:T(4,128)} %bitcast.1, s32[4]{0:T(128)} %phase_bins.1, s32[4]{0:T(128)} %assignment.1, bf16[2,8,32768]{2,1,0:T(8,128)(2,1)} %voltages.1, f32[32,8192]{1,0:T(8,128)} %phase_model.1, bf16[256,256]{1,0:T(8,128)(2,1)} %constant.6.clone.first_hbm, ...), custom_call_target="tpu_custom_call" | custom-call | tf_op jit(solution)/shard_map/correlate/pallas_call | solution.py:728
  65.3 1.1 %convert_element_type.3 = f32[4,4,2,64,128]{4,3,2,1,0:T(8,128)} convert(bf16[4,4,2,64,128]{4,3,2,1,0:T(8,128)(2,1)S(1)} %correlate.1) | non-fusion elementwise | flops 262144 | bytes 1572864 | tf_op jit(solution)/shard_map/convert_element_type | solution.py:738

commit v3 on v2

--- a/solution.py
+++ b/solution.py
@@ -24,6 +24,7 @@
 UNIT = NCHAN // LANES
 AHEAD = DELAY_MAX // NCHAN
 SLICES = GROUP_ST * GROUP_ST // 2
+PART = 32
 F32, BF16, I32 = jnp.float32, jnp.bfloat16, jnp.int32
 MESH = pl.DeviceIdType.MESH
 
@@ -70,7 +71,7 @@
 def fused_kernel(dims, delays, phase_bins, assignment, voltages, phase_model, first_hbm, twist_hbm, second_hbm, out,
                  small, first, twist, second, rxu, series, windows, turned, planes, rows, phases, phase_rows, trig,
                  tx2, rx2, gs, tscr, tx3, rx3, sums, tx4, rx4, landed, rxd, rxb, heard, tables, orders,
-                 load_sems, s0, r0, s1, r1, s2, r2, s3, r3, s4, r4, s5, own_sems, unit_sems):
+                 load_sems, s0, r0, s1, r1, s2, r2, s3, r3, s4, r4, s5, own_sems, unit_sems, crossed):
     owners, pairs, frames, stations, slots = dims
     devices, layers, halves = owners * pairs, owners // 2, pairs // 2
     all_frames = owners * frames
@@ -144,50 +145,54 @@
     def at(layer, half, core):
         return (2 * layer + half, 2 * m + core)
 
-    def sample_copy(index, src, where, slot):
-        return remote(src, rxu.at[slot], s1.at[index], r1.at[slot], where)
-
-    def own_unit(i):
-        return voltages.at[:, :, pl.ds(i * NCHAN, NCHAN)]
-
-    def arrived(slot):
-        sample_copy(0, rxu.at[slot], at(u, h, c), slot).wait_recv()
+    def sample_copy(group, src, where, slot, r):
+        return remote(src, rxu.at[slot, r], s1.at[group], r1.at[slot, r], where)
+
+    def own_unit(i, r):
+        return voltages.at[r, :, pl.ds(i * NCHAN, NCHAN)]
+
+    def own_copy(i, r):
+        return pltpu.make_async_copy(own_unit(i, r), rxu.at[i, r], unit_sems.at[i, r])
+
+    def arrived(slot, r):
+        sample_copy(0, rxu.at[slot, r], at(u, h, c), slot, r).wait_recv()
 
     below = u > 0
     lower = jnp.maximum(u - 1, 0)
     is00, is10 = (h == 0) & (c == 0), (h == 1) & (c == 0)
     is01, is11 = (h == 0) & (c == 1), (h == 1) & (c == 1)
-    start_00 = [(0, 0, (lower, 0, 0), 8), (1, 1, (lower, 0, 0), 9), (2, 2, (lower, 0, 1), 6), (3, 3, (lower, 0, 1), 7)]
+    both = [(i, r) for i in range(4) for r in range(2)]
 
     @pl.when(is10)
     def _():
-        for i in range(4):
-            sample_copy(i, own_unit(i), at(u, 0, 0), 4 + i).start()
+        for i, r in both:
+            sample_copy(0, own_unit(i, r), at(u, 0, 0), 4 + i, r).start()
 
     @pl.when(is01)
     def _():
-        for i in range(4):
-            sample_copy(i, own_unit(i), at(u, 1, 0), i).start()
+        for i, r in both:
+            sample_copy(0, own_unit(i, r), at(u, 1, 0), i, r).start()
 
     @pl.when(is11)
     def _():
-        for i in range(4):
-            sample_copy(i, own_unit(i), at(u, 1, 0), 4 + i).start()
+        for i, r in both:
+            sample_copy(0, own_unit(i, r), at(u, 1, 0), 4 + i, r).start()
 
         @pl.when(below)
         def _():
-            for i in range(2):
-                sample_copy(4 + i, own_unit(i), at(lower, 1, 1), 8 + i).start()
+            for i, r in both[:4]:
+                sample_copy(1, own_unit(i, r), at(lower, 1, 1), 8 + i, r).start()
 
     @pl.when(c == h)
     def _():
-        for i in range(4):
-            pltpu.make_async_copy(own_unit(i), rxu.at[i], unit_sems.at[i]).start()
+        for i, r in both:
+            own_copy(i, r).start()
 
     @pl.when(is00 & below)
     def _():
-        for index, i, where, slot in start_00:
-            sample_copy(index, own_unit(i), at(*where), slot).start()
+        for i, r in both:
+            where, slot = (at(lower, 0, 0), 8 + i) if i < 2 else (at(lower, 0, 1), 4 + i)
+            sample_copy(1, own_unit(i, r), where, slot, r).start()
 
     for copy in loads:
         copy.wait()
@@ -223,13 +228,17 @@
     hear.start()
     hear.wait()
 
-    def widen(slot):
+    def widen(slot, r):
         def one(j, carry):
-            for r in range(2):
-                held = rxu[slot, r, :, pl.ds(pl.multiple_of(j * LANES, LANES), LANES)].astype(F32)
-                series[pl.ds(r * stations * depth + slot * UNIT + j, stations, stride=depth), :] = held
-            return carry
-        lax.fori_loop(0, UNIT, one, 0, unroll=8)
+            held = rxu[slot, r, :, pl.ds(pl.multiple_of(j * LANES, LANES), LANES)].astype(F32)
+            series[pl.ds(r * stations * depth + slot * UNIT + j, stations, stride=depth), :] = held
+            return carry
+        lax.fori_loop(0, UNIT, one, 0, unroll=16)
+
+    def take(slot):
+        for r in range(2):
+            arrived(slot, r)
+            widen(slot, r)
 
     def blank(slot):
         def one(i, carry):
@@ -243,63 +252,66 @@
 
     lax.fori_loop(0, 2 * stations, clear_tail, 0)
 
-    @pl.when(is00)
-    def _():
-        for slot in range(4):
-            pltpu.make_async_copy(own_unit(slot), rxu.at[slot], unit_sems.at[slot]).wait()
-            widen(slot)
-        for slot in range(4, 8):
-            arrived(slot)
-            sample_copy(4 + slot, rxu.at[slot], at(u, 0, 1), slot - 4).start()
+    def cross(slot):
+        for r in range(2):
+            arrived(slot, r)
+            sample_copy(0, rxu.at[slot, r], at(u, 0, 1), slot - 4, r).start()
             if slot < 6:
                 @pl.when(below)
-                def _(slot=slot):
-                    sample_copy(slot, rxu.at[slot], at(lower, 0, 1), slot + 4).start()
+                def _(slot=slot, r=r):
+                    sample_copy(1, rxu.at[slot, r], at(lower, 0, 1), slot + 4, r).start()
 
                 @pl.when(jnp.logical_not(top))
-                def _(slot=slot):
-                    arrived(slot + 4)
-                    sample_copy(slot + 8, rxu.at[slot + 4], at(u, 0, 1), slot).start()
-                    widen(slot + 4)
-            widen(slot)
+                def _(slot=slot, r=r):
+                    arrived(slot + 4, r)
+                    sample_copy(2, rxu.at[slot + 4, r], at(u, 0, 1), slot, r).start()
+                    widen(slot + 4, r)
+            widen(slot, r)
+
+    @pl.when(c == h)
+    def _():
+        for i, r in both:
+            own_copy(i, r).wait()
+            widen(i, r)
+
+    @pl.when(is00)
+    def _():
+        for slot in range(4, 7):
+            cross(slot)
 
     @pl.when(is10)
     def _():
         for slot in range(4):
-            arrived(slot)
-
-            @pl.when(below)
-            def _(slot=slot):
-                where = at(lower, 1, 0) if slot < 2 else at(lower, 1, 1)
-                sample_copy(4 + slot, rxu.at[slot], where, 8 + slot if slot < 2 else 4 + slot).start()
-            if slot >= 2:
-                @pl.when(jnp.logical_not(top))
-                def _(slot=slot):
-                    arrived(slot + 6)
-                    sample_copy(slot + 6, rxu.at[slot + 6], at(u, 1, 1), slot + 2).start()
-                    widen(slot + 6)
-            widen(slot)
+            for r in range(2):
+                arrived(slot, r)
+
+                @pl.when(below)
+                def _(slot=slot, r=r):
+                    where, into = (at(lower, 1, 0), 8 + slot) if slot < 2 else (at(lower, 1, 1), 4 + slot)
+                    sample_copy(1, rxu.at[slot, r], where, into, r).start()
+                if slot >= 2:
+                    @pl.when(jnp.logical_not(top))
+                    def _(slot=slot, r=r):
+                        arrived(slot + 6, r)
+                        sample_copy(2, rxu.at[slot + 6, r], at(u, 1, 1), slot + 2, r).start()
+                        widen(slot + 6, r)
+                widen(slot, r)
         for slot in range(4, 8):
-            arrived(slot)
-            widen(slot)
+            take(slot)
+
+        @pl.when(top)
+        def _():
+            pl.semaphore_signal(crossed, inc=1, device_id=at(u, 1, 1), device_id_type=MESH)
 
     @pl.when(is01)
     def _():
         for slot in range(4):
-            arrived(slot)
-            widen(slot)
-
-    @pl.when(is11)
-    def _():
-        for slot in range(4):
-            pltpu.make_async_copy(own_unit(slot), rxu.at[slot], unit_sems.at[slot]).wait()
-            widen(slot)
+            take(slot)
 
     @pl.when((c == 1) & jnp.logical_not(top))
     def _():
-        for slot in range(4, 8):
-            arrived(slot)
-            widen(slot)
+        for slot in range(4, 7):
+            take(slot)
 
     @pl.when((c == 1) & top)
     def _():
@@ -311,77 +323,70 @@
         for slot in range(8, 10):
             blank(slot)
 
+    @pl.when(is11 & top)
+    def _():
+        pl.semaphore_wait(crossed, 1)
+
     lane16 = lax.broadcasted_iota(I32, (RADIX_A, LANES), 1)
-    batch = 2
-
-    def frame_copy(j):
-        return remote(tx2.at[j], rx2.at[mine], s2.at[0], r2.at[0], (2 * u + (j + 1) // 2 % 2, j % 2 * 2 + c))
+
+    def frame_copy(j, part):
+        rows_of = pl.ds(part * PART, PART)
+        where = (2 * u + (j + 1) // 2 % 2, j % 2 * 2 + c)
+        return remote(tx2.at[j, rows_of], rx2.at[mine, rows_of], s2.at[0], r2.at[part], where)
 
     def own_frame():
         return pltpu.make_async_copy(tx2.at[e], rx2.at[mine], own_sems.at[6])
 
-    def spectra(step, carry):
-        @pl.when((step == 1) & (c == 1) & jnp.logical_not(top))
-        def _():
-            for slot in range(8, 10):
-                arrived(slot)
-                widen(slot)
-
-        def one_frame(i, inner):
-            f = step * batch + i
-            for s in range(stations):
-                offset = f * NCHAN + heard[0, f * stations + s]
-                row, shift = offset // LANES, offset % LANES
-                for r in range(2):
-                    parts = [
-                        pltpu.roll(
-                            series[pl.ds((r * stations + s) * depth + row + q, RADIX_A, stride=QUADS), :],
-                            (LANES - shift) % LANES, 1)
-                        for q in range(QUADS + 1)
-                    ]
-                    for q in range(QUADS):
-                        cut = jnp.where(lane16 < LANES - shift, parts[q], parts[q + 1])
-                        windows[(2 * s + r) * RADIX_A:(2 * s + r + 1) * RADIX_A, q * LANES:(q + 1) * LANES] = cut.astype(BF16)
-            passed = jnp.dot(first[...], windows[...], preferred_element_type=F32)
-            real, imag = passed[:sk], passed[sk:]
-            here = pl.ds(pl.multiple_of(i * sk, sk), sk)
-            turned[here, 0:RADIX_B] = (real * twist[0] + imag * twist[1]).astype(BF16)
-            turned[here, RADIX_B:] = (imag * twist[0] - real * twist[1]).astype(BF16)
-            return inner
-
-        lax.fori_loop(0, batch, one_frame, 0)
+    def spectra(f, carry):
+        @pl.when((f == 1) & is00)
+        def _():
+            cross(7)
+
+        for slot in range(7, 10):
+            @pl.when((f == slot - 6) & (c == 1) & jnp.logical_not(top))
+            def _(slot=slot):
+                take(slot)
+
+        for s in range(stations):
+            offset = f * NCHAN + heard[0, f * stations + s]
+            row, shift = offset // LANES, offset % LANES
+            for r in range(2):
+                parts = [
+                    pltpu.roll(
+                        series[pl.ds((r * stations + s) * depth + row + q, RADIX_A, stride=QUADS), :],
+                        (LANES - shift) % LANES, 1)
+                    for q in range(QUADS + 1)
+                ]
+                for q in range(QUADS):
+                    cut = jnp.where(lane16 < LANES - shift, parts[q], parts[q + 1])
+                    windows[(2 * s + r) * RADIX_A:(2 * s + r + 1) * RADIX_A, q * LANES:(q + 1) * LANES] = cut.astype(BF16)
+        passed = jnp.dot(first[...], windows[...], preferred_element_type=F32)
+        real, imag = passed[:sk], passed[sk:]
+        turned[:, 0:RADIX_B] = (real * twist[0] + imag * twist[1]).astype(BF16)
+        turned[:, RADIX_B:] = (imag * twist[0] - real * twist[1]).astype(BF16)
         for g in range(QUADS):
             channels = jnp.dot(turned[...], second[:, g * 2 * LANES:(g + 1) * 2 * LANES], preferred_element_type=F32)
-            real = channels[:, :LANES].reshape(batch, sk, LANES)
-            imag = channels[:, LANES:].reshape(batch, sk, LANES)
+            real, imag = channels[:, :LANES], channels[:, LANES:]
             cosine, sine = trig[0, g], trig[1, g]
-            turned_re = (real * cosine - imag * sine).reshape(batch * stations, RADIX_A, LANES)
-            turned_im = (real * sine + imag * cosine).reshape(batch * stations, RADIX_A, LANES)
+            turned_re = (real * cosine - imag * sine).reshape(stations, RADIX_A, LANES)
+            turned_im = (real * sine + imag * cosine).reshape(stations, RADIX_A, LANES)
             planes[:, g * RADIX_A:(g + 1) * RADIX_A, :] = turned_re
             planes[:, CHAVG + g * RADIX_A:CHAVG + (g + 1) * RADIX_A, :] = turned_im
-
-        def one_out(i, inner):
-            def flip(s, deep):
-                rows[pl.ds(s, OUTCH, stride=stations), :] = planes[i * stations + s].T
-                return deep
-
-            lax.fori_loop(0, stations, flip, 0, unroll=4)
-            j = step * batch + i
-            tx2[j] = rows[...].astype(BF16).reshape(OUTCH, stations, LANES)
-
-            @pl.when(j == e)
-            def _():
-                own_frame().start()
-
-            @pl.when(j != e)
-            def _():
-                frame_copy(j).start()
-            return inner
-
-        lax.fori_loop(0, batch, one_out, 0)
-        return carry
-
-    lax.fori_loop(0, frames // batch, spectra, 0)
+        for s in range(stations):
+            rows[pl.ds(s, OUTCH, stride=stations), :] = planes[s].T
+        tx2[f] = rows[...].astype(BF16).reshape(OUTCH, stations, LANES)
+
+        @pl.when(f == e)
+        def _():
+            own_frame().start()
+
+        @pl.when(f != e)
+        def _():
+            for part in range(OUTCH // PART):
+                frame_copy(f, part).start()
+        return carry
+
+    lax.fori_loop(0, frames, spectra, 0)
 
     own_bins.wait()
     rest = rxb.at[pl.ds(0, owners - 1)]
@@ -409,11 +414,8 @@
     def _():
         own_frame().wait()
 
-        rest = rx2.at[pl.ds(0, pairs - 1)]
-        remote(rest, rest, s2.at[0], r2.at[0], (tm, pair)).wait_recv()
-
-        def gram(o, carry):
-            row = o % 2 * (OUTCH // 2) + o // 2
+        def gram(row, carry):
+            o = row % (OUTCH // 2) * 2 + row // (OUTCH // 2)
             left = jnp.concatenate([rx2[g, row].astype(F32) for g in range(pairs)], 0)
             swapped = pltpu.roll(left, CHAVG, 1)
             swapped = jnp.where(lane32 < CHAVG, -swapped, swapped)
@@ -423,8 +425,13 @@
             gs[pl.ds(o, half, stride=OUTCH), :] = jnp.where(lane32[:half] < CHAVG, made[:half], made[half:])
             return carry
 
-        lax.fori_loop(0, OUTCH, gram, 0, unroll=16)
-
+        def one_part(part, carry):
+            rest = rx2.at[pl.ds(0, pairs - 1), pl.ds(0, PART)]
+            remote(rest, rest, s2.at[0], r2.at[part], (tm, pair)).wait_recv()
+            lax.fori_loop(0, PART, lambda i, inner: gram(part * PART + i, inner), 0, unroll=16)
+            return carry
+
+        lax.fori_loop(0, OUTCH // PART, one_part, 0)
         def turn(i, carry):
             block = gs[pl.ds(pl.multiple_of(i * OUTCH, OUTCH), OUTCH), :].T * (1.0 / CHAVG)
             for upper in range(2):
@@ -452,7 +459,7 @@
         frame = tm // 2 * 2 * frames + c * frames + e
 
         def send(step, carry):
-            d = (me + step) % SLICES
+            d = (me + SLICES // 2 + step) % SLICES
 
             @pl.when(d != me)
             def _():
@@ -593,52 +600,41 @@
     def _():
         delay_copy().wait_send()
 
-    def sent(index):
-        sample_copy(index, rxu.at[0], at(u, h, c), 0).wait_send()
-
-    @pl.when(is00)
-    def _():
-        for index in range(8, 12):
-            sent(index)
-
-        @pl.when(below)
-        def _():
-            for index in range(6):
-                sent(index)
-
-        @pl.when(jnp.logical_not(top))
-        def _():
-            for index in range(12, 14):
-                sent(index)
-
-    @pl.when(is10)
-    def _():
-        for index in range(4):
-            sent(index)
-
-        @pl.when(below)
-        def _():
-            for index in range(4, 8):
-                sent(index)
-
-        @pl.when(jnp.logical_not(top))
-        def _():
-            for index in range(8, 10):
-                sent(index)
-
-    @pl.when(c == 1)
-    def _():
-        for index in range(4):
-            sent(index)
-
-    @pl.when(is11 & below)
-    def _():
-        for index in range(4, 6):
-            sent(index)
-
     def all_sent(ref, count, sem):
         rest = ref.at[pl.ds(0, count)]
         remote(rest, rest, sem, r4.at[0], (tm, pair)).wait_send()
+
+    @pl.when(is00)
+    def _():
+        all_sent(rxu, 4, s1.at[0])
+
+        @pl.when(below)
+        def _():
+            all_sent(rxu, 6, s1.at[1])
+
+        @pl.when(jnp.logical_not(top))
+        def _():
+            all_sent(rxu, 2, s1.at[2])
+
+    @pl.when(is10)
+    def _():
+        all_sent(rxu, 4, s1.at[0])
+
+        @pl.when(below)
+        def _():
+            all_sent(rxu, 4, s1.at[1])
+
+        @pl.when(jnp.logical_not(top))
+        def _():
+            all_sent(rxu, 2, s1.at[2])
+
+    @pl.when(c == 1)
+    def _():
+        all_sent(rxu, 4, s1.at[0])
+
+    @pl.when(is11 & below)
+    def _():
+        all_sent(rxu, 2, s1.at[1])
 
     @pl.when(e < frames)
     def _():
@@ -677,7 +673,6 @@
     all_frames = owners * frames
     bins_here = BINS // owners
     sk = stations * RADIX_A
-    batch = 2
 
     first, twist, second = section_tables(stations)
     span = (frames + AHEAD) * UNIT
@@ -689,8 +684,8 @@
         pltpu.VMEM((frames + AHEAD, 2, stations, NCHAN), BF16),
         pltpu.VMEM((2 * stations * (span + 8), LANES), F32),
         pltpu.VMEM((2 * sk, RADIX_B), BF16),
-        pltpu.VMEM((batch * sk, 2 * RADIX_B), BF16),
-        pltpu.VMEM((batch * stations, LANES, LANES), F32),
+        pltpu.VMEM((sk, 2 * RADIX_B), BF16),
+        pltpu.VMEM((stations, LANES, LANES), F32),
         pltpu.VMEM((OUTCH * stations, LANES), F32),
         pltpu.VMEM((8, NCHAN), F32),
         pltpu.VMEM((8 * UNIT, LANES), F32),
@@ -713,17 +708,18 @@
         pltpu.SemaphoreType.DMA((4,)),
         pltpu.SemaphoreType.DMA((2,)),
         pltpu.SemaphoreType.DMA((2,)),
-        pltpu.SemaphoreType.DMA((14,)),
-        pltpu.SemaphoreType.DMA((frames + AHEAD,)),
+        pltpu.SemaphoreType.DMA((3,)),
+        pltpu.SemaphoreType.DMA((frames + AHEAD, 2)),
         pltpu.SemaphoreType.DMA((1,)),
-        pltpu.SemaphoreType.DMA((1,)),
+        pltpu.SemaphoreType.DMA((OUTCH // PART,)),
         pltpu.SemaphoreType.DMA((1,)),
         pltpu.SemaphoreType.DMA((1,)),
         pltpu.SemaphoreType.DMA((1,)),
         pltpu.SemaphoreType.DMA((SLICES,)),
         pltpu.SemaphoreType.DMA((1,)),
         pltpu.SemaphoreType.DMA((7,)),
-        pltpu.SemaphoreType.DMA((4,)),
+        pltpu.SemaphoreType.DMA((4, 2)),
+        pltpu.SemaphoreType.REGULAR,
     ]
     result = pl.pallas_call(
         functools.partial(fused_kernel, (owners, pairs, frames, stations, slots)),

time: 66.6 us -> 61.7 us (0.926)
  Pallas kernels: 65.3 us -> 60.4 us
    pallas_call x1, Pallas kernels: 65.3 us -> 60.4 us  [body(): pl.pallas_call(functools.partial(fused_kernel, (owners, pairs, frames, st...]
where the time goes in v3:
time: 61.7 us; the launch traced here: 61.5 us
  Pallas kernels  60.4 us (98%)
  other arithmetic  1.09 us (2%)
    pallas_call x1, Pallas kernels, body(): pl.pallas_call(functools.partial(fused_kernel, (owners, pairs, frames, st...  60.4 us

profile of v3, /device:TPU:0, one launch (start us, length us, event | category | flops | bytes accessed | tf_op | source)
XLA Modules:
  0.0 61.5 jit_solution(10555764444813435568)
XLA Ops:
  0.0 60.4 %correlate.1 = bf16[4,4,2,64,128]{4,3,2,1,0:T(8,128)(2,1)S(1)} custom-call(s32[4,8]{1,0:T(4,128)} %bitcast.1, s32[4]{0:T(128)} %phase_bins.1, s32[4]{0:T(128)} %assignment.1, bf16[2,8,32768]{2,1,0:T(8,128)(2,1)} %voltages.1, f32[32,8192]{1,0:T(8,128)} %phase_model.1, bf16[256,256]{1,0:T(8,128)(2,1)} %constant.6.clone.first_hbm, ...), custom_call_target="tpu_custom_call" | custom-call | tf_op jit(solution)/shard_map/correlate/pallas_call | solution.py:724
  60.4 1.1 %convert_element_type.3 = f32[4,4,2,64,128]{4,3,2,1,0:T(8,128)} convert(bf16[4,4,2,64,128]{4,3,2,1,0:T(8,128)(2,1)S(1)} %correlate.1) | non-fusion elementwise | flops 262144 | bytes 1572864 | tf_op jit(solution)/shard_map/convert_element_type | solution.py:734

commit v4 on v3

--- a/solution.py
+++ b/solution.py
@@ -276,7 +276,7 @@
 
     @pl.when(is00)
     def _():
-        for slot in range(4, 7):
+        for slot in range(4, 8):
             cross(slot)
 
     @pl.when(is10)
@@ -337,13 +337,23 @@
     def own_frame():
         return pltpu.make_async_copy(tx2.at[e], rx2.at[mine], own_sems.at[6])
 
-    def spectra(f, carry):
-        @pl.when((f == 1) & is00)
-        def _():
-            cross(7)
+    def dispatch(f):
+        @pl.when(f == e)
+        def _():
+            own_frame().start()
+
+        @pl.when(f != e)
+        def _():
+            for part in range(OUTCH // PART):
+                frame_copy(f, part).start()
+
+    def spectra(step, carry):
+        there_h = jnp.where(step == 1, h, jnp.where(step == 3, h, 1 - h))
+        there_m = jnp.where((step == 1) | (step == 2), (m + 1) % 2, m)
+        f = jnp.where((c == 0) & (m < 2), (there_h + there_m) % 2 * 2 + there_m, step)
 
         for slot in range(7, 10):
-            @pl.when((f == slot - 6) & (c == 1) & jnp.logical_not(top))
+            @pl.when((step == slot - 6) & (c == 1) & jnp.logical_not(top))
             def _(slot=slot):
                 take(slot)
 
@@ -376,17 +386,23 @@
             rows[pl.ds(s, OUTCH, stride=stations), :] = planes[s].T
         tx2[f] = rows[...].astype(BF16).reshape(OUTCH, stations, LANES)
 
-        @pl.when(f == e)
-        def _():
-            own_frame().start()
-
-        @pl.when(f != e)
-        def _():
-            for part in range(OUTCH // PART):
-                frame_copy(f, part).start()
-        return carry
+        @pl.when(c == 0)
+        def _():
+            dispatch(f)
+
+        @pl.when((c == 1) & (step >= 1))
+        def _():
+            dispatch(step - 1)
+
+        return carry
+
 
     lax.fori_loop(0, frames, spectra, 0)
+
+    @pl.when(c == 1)
+    def _():
+        for j in range(frames - 1, frames):
+            dispatch(j)
 
     own_bins.wait()
     rest = rxb.at[pl.ds(0, owners - 1)]
@@ -492,7 +508,7 @@
             sums[f] = sums[orders[f, 0]] + rx3[f].reshape(2 * NBLK, LANES).astype(F32)
             return carry
 
-        lax.fori_loop(0, all_frames, add, 0)
+        lax.fori_loop(0, all_frames, add, 0, unroll=4)
 
         def gather(b, carry):
             held = sums[orders[all_frames + b, 0]].astype(BF16)

time: 61.7 us -> 59.9 us (0.971)
  Pallas kernels: 60.4 us -> 58.6 us
    pallas_call x1, Pallas kernels: 60.4 us -> 58.6 us  [body(): pl.pallas_call(functools.partial(fused_kernel, (owners, pairs, frames, st...]
where the time goes in v4:
time: 59.9 us; the launch traced here: 59.7 us
  Pallas kernels  58.6 us (98%)
  other arithmetic  1.09 us (2%)
    pallas_call x1, Pallas kernels, body(): pl.pallas_call(functools.partial(fused_kernel, (owners, pairs, frames, st...  58.6 us

profile of v4, /device:TPU:0, one launch (start us, length us, event | category | flops | bytes accessed | tf_op | source)
XLA Modules:
  0.0 59.7 jit_solution(10026587634735831870)
XLA Ops:
  0.0 58.6 %correlate.1 = bf16[4,4,2,64,128]{4,3,2,1,0:T(8,128)(2,1)S(1)} custom-call(s32[4,8]{1,0:T(4,128)} %bitcast.1, s32[4]{0:T(128)} %phase_bins.1, s32[4]{0:T(128)} %assignment.1, bf16[2,8,32768]{2,1,0:T(8,128)(2,1)} %voltages.1, f32[32,8192]{1,0:T(8,128)} %phase_model.1, bf16[256,256]{1,0:T(8,128)(2,1)} %constant.6.clone.first_hbm, ...), custom_call_target="tpu_custom_call" | custom-call | tf_op jit(solution)/shard_map/correlate/pallas_call | solution.py:740
  58.6 1.1 %convert_element_type.3 = f32[4,4,2,64,128]{4,3,2,1,0:T(8,128)} convert(bf16[4,4,2,64,128]{4,3,2,1,0:T(8,128)(2,1)S(1)} %correlate.1) | non-fusion elementwise | flops 262144 | bytes 1572864 | tf_op jit(solution)/shard_map/convert_element_type | solution.py:750

commit v5 on v4

--- a/solution.py
+++ b/solution.py
@@ -24,7 +24,7 @@
 UNIT = NCHAN // LANES
 AHEAD = DELAY_MAX // NCHAN
 SLICES = GROUP_ST * GROUP_ST // 2
-PART = 32
+PART = 16
 F32, BF16, I32 = jnp.float32, jnp.bfloat16, jnp.int32
 MESH = pl.DeviceIdType.MESH
 
@@ -201,7 +201,7 @@
         phase_rows[pl.ds(j, 8, stride=UNIT), :] = phases[:, pl.ds(pl.multiple_of(j * LANES, LANES), LANES)]
         return carry
 
-    lax.fori_loop(0, UNIT, spread, 0)
+    lax.fori_loop(0, UNIT, spread, 0, unroll=8)
     skip = mine * stations % 8
 
     def one_phase(s, carry):
@@ -214,7 +214,7 @@
             trig[1, g, here, :] = sine[g * RADIX_A:(g + 1) * RADIX_A]
         return carry
 
-    lax.fori_loop(0, stations, one_phase, 0)
+    lax.fori_loop(0, stations, one_phase, 0, unroll=2)
 
     @pl.when(c == h)
     def _():
@@ -459,7 +459,7 @@
                         tscr[pl.ds(p * 256 + ri * 128 + a * NGRP + b, GROUP_ST, stride=NBLK), :] = block[top_row:top_row + GROUP_ST]
             return carry
 
-        lax.fori_loop(0, half, turn, 0, unroll=4)
+        lax.fori_loop(0, half, turn, 0, unroll=8)
 
         def pack(p, carry):
             real = tscr[pl.ds(pl.multiple_of(p * 256, 256), 128), :].reshape(GROUP_ST, NBLK, LANES)
@@ -486,9 +486,18 @@
                 pltpu.make_async_copy(tx3.at[d], rx3.at[frame], own_sems.at[3]).start()
             return carry
 
-        lax.fori_loop(0, SLICES, send, 0, unroll=4)
+        lax.fori_loop(0, SLICES, send, 0, unroll=16)
 
     tell.wait()
+
+    def picked(step, order):
+        value = order[0]
+        for i in range(1, len(order)):
+            value = jnp.where(step == i, order[i], value)
+        return value
+
+    def across(k):
+        return (tm + k) % 2 + (tm // 2 + k // 2) % 2 * 2 + (tm // 4 + k // 4) % 2 * 4
 
     @pl.when(me < SLICES)
     def _():
@@ -510,19 +519,18 @@
 
         lax.fori_loop(0, all_frames, add, 0, unroll=4)
 
-        def gather(b, carry):
-            held = sums[orders[all_frames + b, 0]].astype(BF16)
-            tx4[b // bins_here, pl.ds(pl.multiple_of(b % bins_here * 2 * NBLK, 2 * NBLK), 2 * NBLK), :] = held
-            return carry
-
-        lax.fori_loop(0, BINS, gather, 0, unroll=8)
-
-        def send(step, carry):
+        def give(step, carry):
             t = (tm + step) % owners
-            remote(tx4.at[t], rx4.at[me], s4.at[0], r4.at[me], (t, pair)).start()
-            return carry
-
-        lax.fori_loop(1, owners, send, 0)
+            for i in range(bins_here):
+                held = sums[orders[all_frames + t * bins_here + i, 0]].astype(BF16)
+                tx4[t, i * 2 * NBLK:(i + 1) * 2 * NBLK, :] = held
+
+            @pl.when(t != tm)
+            def _():
+                remote(tx4.at[t], rx4.at[me], s4.at[0], r4.at[me], (t, pair)).start()
+            return carry
+
+        lax.fori_loop(1, owners + 1, give, 0, unroll=2)
         pltpu.make_async_copy(tx4.at[tm], rx4.at[me], own_sems.at[4]).start()
 
     sources = SLICES // pairs
@@ -539,9 +547,9 @@
         lax.fori_loop(0, 2 * bins_here, one, 0, unroll=2 * bins_here)
 
     def nearest(step):
-        if sources != 8:
+        if owners != 8:
             return (tm + step) % sources
-        return (tm + step) % 2 + (tm // 2 + step // 2) % 2 * 2 + (tm // 4 + step // 4) % 2 * 4
+        return across(picked(step, (0, 1, 2, 3, 4, 5, 6, 7)))
 
     def first_hop(step, carry):
         i = nearest(step)

time: 59.9 us -> 59.1 us (0.987)
  Pallas kernels: 58.6 us -> 57.8 us
    pallas_call x1, Pallas kernels: 58.6 us -> 57.8 us  [body(): pl.pallas_call(functools.partial(fused_kernel, (owners, pairs, frames, st...]
where the time goes in v5:
time: 59.1 us; the launch traced here: 58.9 us
  Pallas kernels  57.8 us (98%)
  other arithmetic  1.09 us (2%)
    pallas_call x1, Pallas kernels, body(): pl.pallas_call(functools.partial(fused_kernel, (owners, pairs, frames, st...  57.8 us

profile of v5, /device:TPU:0, one launch (start us, length us, event | category | flops | bytes accessed | tf_op | source)
XLA Modules:
  0.0 58.9 jit_solution(16546082309713582772)
XLA Ops:
  0.0 57.8 %correlate.1 = bf16[4,4,2,64,128]{4,3,2,1,0:T(8,128)(2,1)S(1)} custom-call(s32[4,8]{1,0:T(4,128)} %bitcast.1, s32[4]{0:T(128)} %phase_bins.1, s32[4]{0:T(128)} %assignment.1, bf16[2,8,32768]{2,1,0:T(8,128)(2,1)} %voltages.1, f32[32,8192]{1,0:T(8,128)} %phase_model.1, bf16[256,256]{1,0:T(8,128)(2,1)} %constant.6.clone.first_hbm, ...), custom_call_target="tpu_custom_call" | custom-call | tf_op jit(solution)/shard_map/correlate/pallas_call | solution.py:748
  57.9 1.1 %convert_element_type.3 = f32[4,4,2,64,128]{4,3,2,1,0:T(8,128)} convert(bf16[4,4,2,64,128]{4,3,2,1,0:T(8,128)(2,1)S(1)} %correlate.1) | non-fusion elementwise | flops 262144 | bytes 1572864 | tf_op jit(solution)/shard_map/convert_element_type | solution.py:758

commit v6 on v5

--- a/solution.py
+++ b/solution.py
@@ -578,16 +578,19 @@
             remote(rx4.at[d], rx4.at[d], s4.at[0], r4.at[d], (tm, pair)).wait_recv()
             pass_on(d, pair + 1 - 2 * c).start()
             landing(d)
-        return carry
+        beside(i, 0)
+        return carry
+
+    def beside(i, n):
+        d = i * pairs + (pair + 1 - 2 * c + 2 * n) % pairs
+        remote(rx4.at[d], rx4.at[d], s4.at[0], r4.at[d], (tm, pair)).wait_recv()
+        landing(d)
 
     lax.fori_loop(0, sources, second_hop, 0)
 
     def third_hop(step, carry):
-        i = nearest(step)
-        for n in range(halves):
-            d = i * pairs + (pair + 1 - 2 * c + 2 * n) % pairs
-            remote(rx4.at[d], rx4.at[d], s4.at[0], r4.at[d], (tm, pair)).wait_recv()
-            landing(d)
+        for n in range(1, halves):
+            beside(nearest(step), n)
         return carry
 
     lax.fori_loop(0, sources, third_hop, 0)

time: 59.1 us -> 59.1 us (level)
  no operation moved by 1% of the time
where the time goes in v6:
time: 59.1 us; the launch traced here: 58.5 us
  Pallas kernels  57.4 us (97%)
  other arithmetic  1.09 us (2%)
    pallas_call x1, Pallas kernels, body(): pl.pallas_call(functools.partial(fused_kernel, (owners, pairs, frames, st...  57.4 us

profile of v6, /device:TPU:0, one launch (start us, length us, event | category | flops | bytes accessed | tf_op | source)
XLA Modules:
  0.0 58.5 jit_solution(14942556748591075289)
XLA Ops:
  0.0 57.4 %correlate.1 = bf16[4,4,2,64,128]{4,3,2,1,0:T(8,128)(2,1)S(1)} custom-call(s32[4,8]{1,0:T(4,128)} %bitcast.1, s32[4]{0:T(128)} %phase_bins.1, s32[4]{0:T(128)} %assignment.1, bf16[2,8,32768]{2,1,0:T(8,128)(2,1)} %voltages.1, f32[32,8192]{1,0:T(8,128)} %phase_model.1, bf16[256,256]{1,0:T(8,128)(2,1)} %constant.6.clone.first_hbm, ...), custom_call_target="tpu_custom_call" | custom-call | tf_op jit(solution)/shard_map/correlate/pallas_call | solution.py:751
  57.4 1.1 %convert_element_type.3 = f32[4,4,2,64,128]{4,3,2,1,0:T(8,128)} convert(bf16[4,4,2,64,128]{4,3,2,1,0:T(8,128)(2,1)S(1)} %correlate.1) | non-fusion elementwise | flops 262144 | bytes 1572864 | tf_op jit(solution)/shard_map/convert_element_type | solution.py:761

commit v7 on v6

--- a/solution.py
+++ b/solution.py
@@ -614,8 +614,8 @@
                 real = jnp.where(upper, straight, mirrored)
                 imag = jnp.where(upper, -mirrored, straight)
                 imag = jnp.where(within & (place == p), 0.0, imag)
-                out[b, k, 0, p * GROUP_ST:(p + 1) * GROUP_ST, :] = real.astype(BF16)
-                out[b, k, 1, p * GROUP_ST:(p + 1) * GROUP_ST, :] = imag.astype(BF16)
+                out[b, k, 0, p * GROUP_ST:(p + 1) * GROUP_ST, :] = real
+                out[b, k, 1, p * GROUP_ST:(p + 1) * GROUP_ST, :] = imag
         return carry
 
     lax.fori_loop(0, bins_here, one_bin, 0)
@@ -750,7 +750,7 @@
     ]
     result = pl.pallas_call(
         functools.partial(fused_kernel, (owners, pairs, frames, stations, slots)),
-        out_shape=pltpu.VMEM((bins_here, slots, 2, GROUP_ST * GROUP_ST, OUTCH), BF16),
+        out_shape=pltpu.VMEM((bins_here, slots, 2, GROUP_ST * GROUP_ST, OUTCH), F32),
         in_specs=[SMEM, SMEM, SMEM, ANY, ANY, ANY, ANY, ANY],
         out_specs=VMEM,
         scratch_shapes=scratch,
@@ -758,7 +758,7 @@
             collective_id=0, has_side_effects=True, vmem_limit_bytes=56 * 1024 * 1024),
         name="correlate",
     )(delays.T, phase_bins, assignment, voltages, phase_model, first, twist, second)
-    return result.astype(F32)
+    return result
 
 
 def solution(mesh):

time: 59.1 us -> 59 us (level)
  other arithmetic: 1.09 us -> 0 us
  local copies, waits for them, and re-layouts: 0 us -> 0.97 us
    convert_element_type x1 -> x0, other arithmetic: 1.09 us -> none  [body(): return result.astype(F32)]
    unnamed x0 -> x1, local copies, waits for them, and re-layouts: none -> 0.97 us
where the time goes in v7:
time: 59 us; the launch traced here: 58.3 us
  Pallas kernels  57.4 us (97%)
  local copies, waits for them, and re-layouts  0.97 us (2%)
    pallas_call x1, Pallas kernels, body(): pl.pallas_call(functools.partial(fused_kernel, (owners, pairs, frames, st...  57.4 us

profile of v7, /device:TPU:0, one launch (start us, length us, event | category | flops | bytes accessed | tf_op | source)
XLA Modules:
  0.0 58.3 jit_solution(15509419770154075722)
XLA Ops:
  0.0 57.4 %correlate.1 = f32[4,4,2,64,128]{4,3,2,1,0:T(8,128)S(1)} custom-call(s32[4,8]{1,0:T(4,128)} %bitcast.1, s32[4]{0:T(128)} %phase_bins.1, s32[4]{0:T(128)} %assignment.1, bf16[2,8,32768]{2,1,0:T(8,128)(2,1)} %voltages.1, f32[32,8192]{1,0:T(8,128)} %phase_model.1, bf16[256,256]{1,0:T(8,128)(2,1)} %constant.6.clone.first_hbm, ...), custom_call_target="tpu_custom_call" | custom-call | tf_op jit(solution)/shard_map/correlate/pallas_call | solution.py:751
  57.4 1.0 %copy.10 = f32[4,4,2,64,128]{4,3,2,1,0:T(8,128)} copy(f32[4,4,2,64,128]{4,3,2,1,0:T(8,128)S(1)} %correlate.1) | data formatting | bytes 2097152

commit v8 on v7

--- a/solution.py
+++ b/solution.py
@@ -102,6 +102,13 @@
     for copy in loads:
         copy.start()
 
+    barrier = pltpu.get_barrier_semaphore()
+
+    def greet(step, carry):
+        pl.semaphore_signal(barrier, inc=1, device_id=place_of((me + step) % devices), device_id_type=MESH)
+        return carry
+
+    lax.fori_loop(1, devices, greet, 0, unroll=True) if devices < 64 else lax.fori_loop(1, devices, greet, 0)
     lane = lax.broadcasted_iota(I32, (1, LANES), 1)
     listed, marked = jnp.zeros((1, LANES), I32), jnp.zeros((1, LANES), I32)
     for i in range(stations * frames):
@@ -110,14 +117,6 @@
         marked = jnp.where(lane == tm * frames + i, phase_bins[i] + 1, marked)
     small[0] = listed
     small[1] = marked
-
-    barrier = pltpu.get_barrier_semaphore()
-
-    def greet(step, carry):
-        pl.semaphore_signal(barrier, inc=1, device_id=place_of((me + step) % devices), device_id_type=MESH)
-        return carry
-
-    lax.fori_loop(1, devices, greet, 0, unroll=True) if devices < 64 else lax.fori_loop(1, devices, greet, 0)
     pl.semaphore_wait(barrier, devices - 1)
 
     def delay_copy():

time: 59 us -> 59 us (level)
  no operation moved by 1% of the time
where the time goes in v8:
time: 59 us; the launch traced here: 58.3 us
  Pallas kernels  57.3 us (97%)
  local copies, waits for them, and re-layouts  0.97 us (2%)
    pallas_call x1, Pallas kernels, body(): pl.pallas_call(functools.partial(fused_kernel, (owners, pairs, frames, st...  57.3 us

profile of v8, /device:TPU:0, one launch (start us, length us, event | category | flops | bytes accessed | tf_op | source)
XLA Modules:
  0.0 58.3 jit_solution(18033559623719298749)
XLA Ops:
  0.0 57.3 %correlate.1 = f32[4,4,2,64,128]{4,3,2,1,0:T(8,128)S(1)} custom-call(s32[4,8]{1,0:T(4,128)} %bitcast.1, s32[4]{0:T(128)} %phase_bins.1, s32[4]{0:T(128)} %assignment.1, bf16[2,8,32768]{2,1,0:T(8,128)(2,1)} %voltages.1, f32[32,8192]{1,0:T(8,128)} %phase_model.1, bf16[256,256]{1,0:T(8,128)(2,1)} %constant.6.clone.first_hbm, ...), custom_call_target="tpu_custom_call" | custom-call | tf_op jit(solution)/shard_map/correlate/pallas_call | solution.py:750
  57.3 1.0 %copy.10 = f32[4,4,2,64,128]{4,3,2,1,0:T(8,128)} copy(f32[4,4,2,64,128]{4,3,2,1,0:T(8,128)S(1)} %correlate.1) | data formatting | bytes 2097152
